TPU v7x, 32 devices: a whole 2x2x4 slice. The times are simulated.
32 devices in a mesh: rep: 2 (over x), ctx: 16 (over z, y, core).
Axes of the slice: x: 2, y: 2, z: 4, core: 2. Of those that a mesh axis runs over, the one named last changes fastest.
Arguments:
- queries: bfloat16 [4096, 32, 128], P(('rep', 'ctx')), parts along dimension 0, may hold values from -128 to 128
- keys: bfloat16 [4096, 2, 128], P(('rep', 'ctx')), parts along dimension 0, may hold values from -5 to 5
- values: bfloat16 [4096, 2, 128], P(('rep', 'ctx')), parts along dimension 0, may hold values from -6 to 6
- grad_out: bfloat16 [4096, 32, 128], P(('rep', 'ctx')), parts along dimension 0, may hold values from -6 to 6
- selected: int32 [4096, 2, 8], P(('rep', 'ctx')), parts along dimension 0, may hold values from 0 to 31, as said below
Outputs:
- dquery: bfloat16 [4096, 32, 128], P(('rep', 'ctx')), parts along dimension 0
- key_grad: bfloat16 [4096, 2, 128], P(('rep', 'ctx')), parts along dimension 0
- value_grad: bfloat16 [4096, 2, 128], P(('rep', 'ctx')), parts along dimension 0
There are 2 independent parts, one for each index of `rep`. A program takes and returns all parts, laid end to end along the dimension named above; each array names one. Nothing has to cross between parts.
Inputs may be any that keep to these rules, and one draw needn't show every extreme that they name: The 8 blocks of selected[t, g] are different and include block t // 64 and block 0. Over the 128 tokens of one device of ctx, the blocks named for one group that lie on other devices number exactly 7, at most one of each other device; block 0 is among them for every device but the first.
All inputs are finite; a program needn't handle non-finite values.
Results may differ from a plain program's by a relative error of at most 0.0075.
Values may be sent and summed in bfloat16 or wider, within the bound.
A program may use at most 128 MiB of HBM per device.

v0:
```python
import math

import jax
import jax.numpy as jnp
from jax import lax
from jax.sharding import PartitionSpec as P

BLK = 64


def attend_group(query_grp, upstream_grp, pool_keys, pool_values, allowed, block_rows):
    tokens, per_group, head_dim = query_grp.shape
    key_count = pool_keys.shape[0]
    scaling = 1.0 / math.sqrt(head_dim)
    step_count = tokens // block_rows
    query_blocks = query_grp.reshape(step_count, block_rows * per_group, head_dim)
    upstream_blocks = upstream_grp.reshape(step_count, block_rows * per_group, head_dim)
    mask_blocks = allowed.reshape(step_count, block_rows, key_count)
    contract_rows = (((0,), (0,)), ((), ()))
    contract_last = (((1,), (1,)), ((), ()))

    def visit(carry, inputs):
        key_acc, value_acc = carry
        query_rows, upstream_rows, mask_rows = inputs
        scores = lax.dot_general(
            query_rows, pool_keys, contract_last, preferred_element_type=jnp.float32
        )
        scores = scores.reshape(block_rows, per_group, key_count) * scaling
        scores = jnp.where(mask_rows[:, None, :], scores, -jnp.inf)
        row_peak = jnp.max(scores, axis=-1, keepdims=True)
        weights = jnp.exp(scores - row_peak)
        weights = weights / jnp.sum(weights, axis=-1, keepdims=True)
        slope_grad = lax.dot_general(
            upstream_rows, pool_values, contract_last, preferred_element_type=jnp.float32
        )
        slope_grad = slope_grad.reshape(block_rows, per_group, key_count)
        row_inner = jnp.sum(weights * slope_grad, axis=-1, keepdims=True)
        dscore = (weights * (slope_grad - row_inner) * scaling).astype(jnp.bfloat16)
        dscore = dscore.reshape(block_rows * per_group, key_count)
        weights_low = weights.astype(jnp.bfloat16).reshape(block_rows * per_group, key_count)
        dquery = jnp.dot(dscore, pool_keys, preferred_element_type=jnp.float32).astype(jnp.bfloat16)
        key_acc = key_acc + lax.dot_general(
            dscore, query_rows, contract_rows, preferred_element_type=jnp.float32
        )
        value_acc = value_acc + lax.dot_general(
            weights_low, upstream_rows, contract_rows, preferred_element_type=jnp.float32
        )
        return ((key_acc, value_acc), dquery)

    zeros_init = jnp.zeros((key_count, head_dim), jnp.float32)
    (key_acc, value_acc), dquery = lax.scan(
        visit, (zeros_init, zeros_init), (query_blocks, upstream_blocks, mask_blocks)
    )
    return (dquery.reshape(tokens, per_group, head_dim), key_acc, value_acc)


def local(queries, keys, values, grad_out, selected):
    tokens, head_count, head_dim = queries.shape
    groups = keys.shape[1]
    per_group = head_count // groups
    block_len = BLK
    own_blocks = tokens // block_len
    owners = lax.axis_size("ctx")
    fetched = min(owners - 2, max(selected.shape[2] - own_blocks, 4)) + 1
    block_rows = min(tokens, 128)
    my_index = lax.axis_index("ctx")
    peer_ids = jnp.arange(owners)
    owner_of = selected // own_blocks
    local_of = selected % own_blocks
    matches = owner_of[..., None] == peer_ids
    wanted = jnp.any(matches, axis=(0, 2)) & (peer_ids[None, :] != my_index)
    local_ids = jnp.max(jnp.where(matches, local_of[..., None], 0), axis=(0, 2))
    block_table = local_ids.T
    live_table = wanted.T.astype(jnp.int32)
    asked_block, asked_live = (
        lax.all_to_all(block_table, "ctx", split_axis=0, concat_axis=0, tiled=True),
        lax.all_to_all(live_table, "ctx", split_axis=0, concat_axis=0, tiled=True),
    )
    stacked = jnp.stack([keys, values], axis=2)
    own_items = stacked.reshape(own_blocks, block_len, groups, 2, head_dim).transpose(0, 2, 3, 1, 4)
    outgoing_tiles = own_items[asked_block, jnp.arange(groups)[None, :]]
    outgoing_tiles = jnp.where(
        asked_live[:, :, None, None, None] > 0, outgoing_tiles, jnp.zeros((), jnp.bfloat16)
    )
    arrived = lax.all_to_all(outgoing_tiles, "ctx", split_axis=0, concat_axis=0, tiled=True)
    query_pos = my_index * tokens + jnp.arange(tokens)
    own_ids = my_index * own_blocks + jnp.arange(own_blocks)
    dquery_parts = []
    own_grads = []
    back_parts = []
    for group in range(groups):
        is_live = wanted[group]
        slot_pos = jnp.cumsum(is_live.astype(jnp.int32)) - 1
        picker = (slot_pos[None, :] == jnp.arange(fetched)[:, None]) & is_live[None, :]
        far_blocks = jnp.sum(
            jnp.where(picker, peer_ids[None, :] * own_blocks + local_ids[group][None, :], 0), axis=1
        )
        fetched_kv = jnp.dot(
            picker.astype(jnp.bfloat16),
            arrived[:, group].reshape(owners, -1),
            preferred_element_type=jnp.float32,
        )
        fetched_kv = fetched_kv.astype(jnp.bfloat16).reshape(fetched, 2, block_len, head_dim)
        pool_kv = jnp.concatenate([own_items[:, group], fetched_kv], axis=0)
        pool_blocks = jnp.concatenate([own_ids, far_blocks], axis=0)
        pool_keys = pool_kv[:, 0].reshape(-1, head_dim)
        pool_values = pool_kv[:, 1].reshape(-1, head_dim)
        key_pos = (pool_blocks[:, None] * block_len + jnp.arange(block_len)[None, :]).reshape(-1)
        picked = jnp.any(selected[:, group, :, None] == pool_blocks[None, None, :], axis=1)
        allowed = jnp.repeat(picked, block_len, axis=1) & (key_pos[None, :] <= query_pos[:, None])
        lower = group * per_group
        dquery, key_acc, value_acc = attend_group(
            queries[:, lower : lower + per_group],
            grad_out[:, lower : lower + per_group],
            pool_keys,
            pool_values,
            allowed,
            block_rows,
        )
        pool_grads = (
            jnp.stack([key_acc, value_acc], axis=0)
            .reshape(2, -1, block_len, head_dim)
            .transpose(1, 0, 2, 3)
        )
        own_grads.append(pool_grads[:own_blocks])
        back_parts.append(
            jnp.dot(
                picker.astype(jnp.float32).T,
                pool_grads[own_blocks:].reshape(fetched, -1),
                precision=lax.Precision.HIGHEST,
            )
        )
        dquery_parts.append(dquery)
    outgoing = jnp.stack(back_parts, axis=1).reshape(owners, groups, 2, block_len, head_dim)
    returned = lax.all_to_all(outgoing, "ctx", split_axis=0, concat_axis=0, tiled=True)
    collected = []
    for group in range(groups):
        senders = (asked_block[:, group][None, :] == jnp.arange(own_blocks)[:, None]) & (
            asked_live[:, group][None, :] > 0
        )
        summed = jnp.dot(
            senders.astype(jnp.float32),
            returned[:, group].reshape(owners, -1),
            precision=lax.Precision.HIGHEST,
        )
        collected.append(summed.reshape(own_blocks, 2, block_len, head_dim) + own_grads[group])
    summed_all = jnp.stack(collected, axis=1)
    key_grad = (
        summed_all[:, :, 0]
        .transpose(0, 2, 1, 3)
        .reshape(tokens, groups, head_dim)
        .astype(jnp.bfloat16)
    )
    value_grad = (
        summed_all[:, :, 1]
        .transpose(0, 2, 1, 3)
        .reshape(tokens, groups, head_dim)
        .astype(jnp.bfloat16)
    )
    dquery_all = jnp.concatenate(dquery_parts, axis=1)
    return (dquery_all, key_grad, value_grad)


def solution(mesh):
    return jax.shard_map(
        local,
        mesh=mesh,
        in_specs=(
            P(("rep", "ctx"), None, None),
            P(("rep", "ctx"), None, None),
            P(("rep", "ctx"), None, None),
            P(("rep", "ctx"), None, None),
            P(("rep", "ctx"), None, None),
        ),
        out_specs=(
            P(("rep", "ctx"), None, None),
            P(("rep", "ctx"), None, None),
            P(("rep", "ctx"), None, None),
        ),
        check_vma=False,
    )
```

profile of v0, /device:TPU:15, one launch (start us, length us, event | category | flops | bytes accessed | tf_op | source)
XLA Modules:
  0.0 237.0 jit_solution(14065132021041090057)
XLA Ops:
  0.6 0.8 add_select_fusion.1
  1.5 0.7 copy.167
  2.2 6.5 %all-to-all-start.1 = ((s32[16,1,2]{2,1,0:T(1,128)}), s32[16,1,2]{2,1,0:T(1,128)S(1)}, u32[]{:S(2)}, u32[]{:S(2)}) async-start(s32[16,1,2]{2,1,0:T(1,128)} %copy.167), calls=%async_computation.1 | async-start | bytes 16384 | tf_op jit(solution)/shard_map/all_to_all | solution.py:76
  9.4 0.9 copy.162
  10.3 0.9 copy.163
  11.3 0.7 copy.164
  12.6 6.0 %all-to-all-start = ((s32[16,1,2]{2,1,0:T(1,128)}), s32[16,1,2]{2,1,0:T(1,128)S(1)}, u32[]{:S(2)}, u32[]{:S(2)}) async-start(s32[16,1,2]{2,1,0:T(1,128)} %copy.164), calls=%async_computation | async-start | bytes 16384 | tf_op jit(solution)/shard_map/all_to_all | solution.py:77
  18.8 3.6 %all-to-all-done = s32[16,1,2]{2,1,0:T(1,128)S(1)} async-done(((s32[16,1,2]{2,1,0:T(1,128)}), s32[16,1,2]{2,1,0:T(1,128)S(1)}, u32[]{:S(2)}, u32[]{:S(2)}) %all-to-all-start) | async-done | bytes 160 | tf_op jit(solution)/shard_map/all_to_all | solution.py:77
  23.1 0.7 gather_fusion
  23.8 1.1 broadcast_select_fusion.2
  24.9 6.8 %all-to-all-start.2 = ((bf16[16,2,2,64,128]{4,3,2,1,0:T(8,128)(2,1)}), bf16[16,2,2,64,128]{4,3,2,1,0:T(8,128)(2,1)}, u32[]{:S(2)}, u32[]{:S(2)}) async-start(bf16[16,2,2,64,128]{4,3,2,1,0:T(8,128)(2,1)} %broadcast_select_fusion.2), calls=%async_computation.2 | async-start | bytes 2097152 | tf_op jit(solution)/shard_map/all_to_all | solution.py:85
  33.3 1.4 copy.179
  35.1 1.4 copy.172
  36.6 0.6 slice_bitcast_fusion.1
  37.2 1.4 fusion.89
  38.6 1.1 fusion.90
  39.8 16.9 %all-to-all-done.2 = bf16[16,2,2,64,128]{4,3,2,1,0:T(8,128)(2,1)} async-done(((bf16[16,2,2,64,128]{4,3,2,1,0:T(8,128)(2,1)}), bf16[16,2,2,64,128]{4,3,2,1,0:T(8,128)(2,1)}, u32[]{:S(2)}, u32[]{:S(2)}) %all-to-all-start.2) | async-done | bytes 1048608 | tf_op jit(solution)/shard_map/all_to_all | solution.py:85
  56.7 1.3 fusion.91
  58.0 1.1 fusion.32
  59.1 1.0 fusion.33
  60.2 1.6 pad_maximum_fusion.2
  61.7 0.7 copy-done.5
  62.4 3.7 %fusion.18 = (f32[2048]{0:T(1024)}, f32[2048,576]{0,1:T(8,128)}) fusion(pred[2048,576]{0,1:T(32,128)(4,1)S(1)} %copy.172, bf16[576,128]{1,0:T(8,128)(2,1)S(1)} %bitcast.258, bf16[2048,128]{1,0:T(8,128)(2,1)S(1)} %bitcast.247), kind=kOutput, calls=%fused_computation.41 | convolution fusion | flops 305526784 | bytes 6578176 | tf_op jit(solution)/shard_map/while/body/eval_jaxpr/dot_general | solution.py:25
  66.1 0.8 sub.109
  66.9 4.0 %fusion.1 = f32[2048]{0:T(1024)} fusion(f32[2048]{0:T(1024)} %get-tuple-element.120, pred[2048,576]{0,1:T(32,128)(4,1)S(1)} %copy.172, f32[2048,576]{0,1:T(8,128)} %get-tuple-element.121), kind=kLoop, calls=%fused_computation.16 | loop fusion | flops 3536896 | bytes 5914624 | tf_op jit(solution)/shard_map/while/body/eval_jaxpr/reduce_sum | solution.py:32
  70.9 5.8 %copy.183 = f32[2048,576]{1,0:T(8,128)} copy(f32[2048,576]{0,1:T(8,128)} %get-tuple-element.121) | data formatting | bytes 9437184 | tf_op jit(solution)/shard_map/while/body/eval_jaxpr/mul | solution.py:28
  76.7 4.6 %fusion.19 = (f32[2048]{0:T(1024)}, f32[2048,576]{0,1:T(8,128)}) fusion(pred[2048,576]{0,1:T(32,128)(4,1)S(1)} %copy.179, bf16[576,128]{1,0:T(8,128)(2,1)} %bitcast.256, bf16[2048,128]{1,0:T(8,128)(2,1)S(1)} %bitcast.246), kind=kOutput, calls=%fused_computation.42 | convolution fusion | flops 305526784 | bytes 6578176 | tf_op jit(solution)/shard_map/while/body/eval_jaxpr/dot_general | solution.py:25
  81.2 1.4 sub.115
  82.6 4.0 %fusion.3 = f32[2048]{0:T(1024)} fusion(f32[2048]{0:T(1024)} %get-tuple-element.116, pred[2048,576]{0,1:T(32,128)(4,1)S(1)} %copy.179, f32[2048,576]{0,1:T(8,128)} %get-tuple-element.117), kind=kLoop, calls=%fused_computation.18 | loop fusion | flops 3536896 | bytes 5914624 | tf_op jit(solution)/shard_map/while/body/eval_jaxpr/reduce_sum | solution.py:32
  86.7 5.8 %copy.190 = f32[2048,576]{1,0:T(8,128)} copy(f32[2048,576]{0,1:T(8,128)} %get-tuple-element.117) | data formatting | bytes 9437184 | tf_op jit(solution)/shard_map/while/body/eval_jaxpr/mul | solution.py:28
  92.4 1.4 div.57
  93.8 6.9 %multiply_reduce_fusion.1 = (f32[2048]{0:T(1024)}, f32[2048,576]{0,1:T(8,128)}) fusion(f32[2048]{0:T(1024)} %fusion.1, f32[2048]{0:T(1024)} %get-tuple-element.120, pred[2048,576]{0,1:T(32,128)(4,1)S(1)} %copy.172, f32[2048,576]{0,1:T(8,128)} %get-tuple-element.121, bf16[576,128]{1,0:T(8,128)(2,1)} %bitcast.267, bf16[2048,128]{1,0:T(8,128)(2,1)} %bitcast.261), kind=kOutput, calls=%fused_computation.12 | convolution fusion | flops 307886080 | bytes 11313152 | tf_op jit(solution)/shard_map/while/body/eval_jaxpr/dot_general | solution.py:33
  100.7 1.4 sub.112
  102.1 5.8 %copy.184 = f32[2048,576]{1,0:T(8,128)} copy(f32[2048,576]{0,1:T(8,128)} %get-tuple-element.123) | data formatting | bytes 9437184 | tf_op jit(solution)/shard_map/while/body/eval_jaxpr/dot_general | solution.py:33
  107.9 6.7 %fusion.4 = (bf16[576,128,16]{0,2,1:T(8,128)(2,1)}, bf16[576,128,16]{0,2,1:T(8,128)(2,1)}) fusion(f32[128,16,576]{2,1,0:T(8,128)} %bitcast.233, f32[128,16]{1,0:T(8,128)} %sub.112, f32[128,16]{1,0:T(8,128)} %div.57, f32[128,16]{1,0:T(8,128)S(1)} %sub.109, f32[128,16,576]{2,1,0:T(8,128)} %bitcast.232, pred[128,576]{1,0:T(8,128)(4,1)} %copy-done.3), kind=kLoop, calls=%fused_computation.21 | loop fusion | flops 9437184 | bytes 14254080 | tf_op jit(solution)/shard_map/while/body/eval_jaxpr/dot_general | solution.py:42
  114.6 5.2 %copy.185 = bf16[576,128,16]{1,2,0:T(8,128)(2,1)} copy(bf16[576,128,16]{0,2,1:T(8,128)(2,1)} %get-tuple-element.78) | data formatting | bytes 4718592 | tf_op jit(solution)/shard_map/while/body/eval_jaxpr/dot_general | solution.py:42
  119.7 3.2 %fusion.20 = f32[1,9,64,128]{3,2,1,0:T(8,128)} fusion(bf16[9,64,128,16]{2,3,1,0:T(8,128)(2,1)} %bitcast.242, bf16[128,16,128]{2,1,0:T(8,128)(2,1)S(1)} %get-tuple-element.84), kind=kOutput, calls=%fused_computation.46 | convolution fusion | flops 301989888 | bytes 3178496 | tf_op jit(solution)/shard_map/while/body/eval_jaxpr/dot_general | solution.py:42
  122.9 5.2 %copy.187 = bf16[576,128,16]{1,2,0:T(8,128)(2,1)} copy(bf16[576,128,16]{0,2,1:T(8,128)(2,1)} %get-tuple-element.79) | data formatting | bytes 4718592 | tf_op jit(solution)/shard_map/while/body/eval_jaxpr/dot_general | solution.py:45
  128.2 2.5 %fusion.23 = f32[1,9,64,128]{3,2,1,0:T(8,128)S(1)} fusion(bf16[9,64,128,16]{2,3,1,0:T(8,128)(2,1)} %bitcast.243, bf16[128,16,128]{2,1,0:T(8,128)(2,1)S(1)} %copy-done.7), kind=kOutput, calls=%fused_computation.47 | convolution fusion | flops 301989888 | bytes 3178496 | tf_op jit(solution)/shard_map/while/body/eval_jaxpr/dot_general | solution.py:45
  130.6 1.0 maximum_bitcast_fusion
  132.0 1.6 convolution_bitcast_fusion.3
  133.6 1.4 div.60
  135.1 6.9 %multiply_reduce_fusion = (f32[2048]{0:T(1024)}, f32[2048,576]{0,1:T(8,128)}) fusion(f32[2048]{0:T(1024)} %fusion.3, f32[2048]{0:T(1024)} %get-tuple-element.116, pred[2048,576]{0,1:T(32,128)(4,1)S(1)} %copy.179, f32[2048,576]{0,1:T(8,128)} %get-tuple-element.117, bf16[576,128]{1,0:T(8,128)(2,1)} %bitcast.266, bf16[2048,128]{1,0:T(8,128)(2,1)} %bitcast.260), kind=kOutput, calls=%fused_computation.8 | convolution fusion | flops 307886080 | bytes 11313152 | tf_op jit(solution)/shard_map/while/body/eval_jaxpr/dot_general | solution.py:33
  141.9 1.4 sub.118
  143.3 5.8 %copy.191 = f32[2048,576]{1,0:T(8,128)} copy(f32[2048,576]{0,1:T(8,128)} %get-tuple-element.119) | data formatting | bytes 9437184 | tf_op jit(solution)/shard_map/while/body/eval_jaxpr/dot_general | solution.py:33
  149.1 6.7 %fusion.5 = (bf16[576,128,16]{0,2,1:T(8,128)(2,1)}, bf16[576,128,16]{0,2,1:T(8,128)(2,1)}) fusion(f32[128,16,576]{2,1,0:T(8,128)} %bitcast.234, f32[128,16]{1,0:T(8,128)} %sub.118, f32[128,16]{1,0:T(8,128)} %div.60, f32[128,16]{1,0:T(8,128)} %sub.115, f32[128,16,576]{2,1,0:T(8,128)} %bitcast.231, pred[128,576]{1,0:T(8,128)(4,1)S(1)} %copy.176), kind=kLoop, calls=%fused_computation.22 | loop fusion | flops 9437184 | bytes 14254080 | tf_op jit(solution)/shard_map/while/body/eval_jaxpr/dot_general | solution.py:42
  155.8 5.2 %copy.192 = bf16[576,128,16]{1,2,0:T(8,128)(2,1)} copy(bf16[576,128,16]{0,2,1:T(8,128)(2,1)} %get-tuple-element.80) | data formatting | bytes 4718592 | tf_op jit(solution)/shard_map/while/body/eval_jaxpr/dot_general | solution.py:42
  161.0 3.2 %fusion.26 = f32[1,9,64,128]{3,2,1,0:T(8,128)} fusion(bf16[9,64,128,16]{2,3,1,0:T(8,128)(2,1)} %bitcast.244, bf16[128,16,128]{2,1,0:T(8,128)(2,1)S(1)} %get-tuple-element.85), kind=kOutput, calls=%fused_computation.48 | convolution fusion | flops 301989888 | bytes 3178496 | tf_op jit(solution)/shard_map/while/body/eval_jaxpr/dot_general | solution.py:42
  164.2 5.2 %copy.194 = bf16[576,128,16]{1,2,0:T(8,128)(2,1)} copy(bf16[576,128,16]{0,2,1:T(8,128)(2,1)} %get-tuple-element.81) | data formatting | bytes 4718592 | tf_op jit(solution)/shard_map/while/body/eval_jaxpr/dot_general | solution.py:45
  169.4 2.5 %fusion.29 = f32[1,9,64,128]{3,2,1,0:T(8,128)S(1)} fusion(bf16[9,64,128,16]{2,3,1,0:T(8,128)(2,1)} %bitcast.245, bf16[128,16,128]{2,1,0:T(8,128)(2,1)S(1)} %copy-done.6), kind=kOutput, calls=%fused_computation.49 | convolution fusion | flops 301989888 | bytes 3178496 | tf_op jit(solution)/shard_map/while/body/eval_jaxpr/dot_general | solution.py:45
  172.0 1.0 maximum_bitcast_fusion.1
  173.8 0.7 convolution_bitcast_fusion.2
  174.7 2.0 copy.197
  176.6 4.9 %all-to-all-start.3 = ((f32[16,2,2,64,128]{4,3,2,1,0:T(8,128)}), f32[16,2,2,64,128]{4,3,2,1,0:T(8,128)}, u32[]{:S(2)}, u32[]{:S(2)}) async-start(f32[16,2,2,64,128]{4,3,2,1,0:T(8,128)} %copy.197), calls=%async_computation.3 | async-start | bytes 4194304 | tf_op jit(solution)/shard_map/all_to_all | solution.py:135
  181.7 6.0 %convolution_convert_fusion.3 = bf16[2048,128]{1,0:T(8,128)(2,1)S(1)} fusion(bf16[576,128]{1,0:T(8,128)(2,1)} %bitcast.259, f32[2048,576]{0,1:T(8,128)} %get-tuple-element.123, f32[2048]{0:T(1024)S(1)} %copy-done.23, f32[2048]{0:T(1024)S(1)} %copy-done.10, f32[2048]{0:T(1024)S(1)} %copy-done.8, pred[2048,576]{0,1:T(32,128)(4,1)S(1)} %copy.172, ...), kind=kOutput, calls=%fused_computation.26 | convolution fusion | flops 310509568 | bytes 11313152 | tf_op jit(solution)/shard_map/while/body/eval_jaxpr/dot_general | solution.py:41
  187.8 4.4 %convolution_convert_fusion.2 = bf16[2048,128]{1,0:T(8,128)(2,1)S(1)} fusion(bf16[576,128]{1,0:T(8,128)(2,1)S(1)} %bitcast.257, f32[2048,576]{0,1:T(8,128)} %get-tuple-element.119, f32[2048]{0:T(1024)S(1)} %copy-done.24, f32[2048]{0:T(1024)S(1)} %copy-done.11, f32[2048]{0:T(1024)S(1)} %copy-done.9, pred[2048,576]{0,1:T(32,128)(4,1)S(1)} %copy.179, ...), kind=kOutput, calls=%fused_computation.25 | convolution fusion | flops 310509568 | bytes 11313152 | tf_op jit(solution)/shard_map/while/body/eval_jaxpr/dot_general | solution.py:41
  192.2 1.1 pad_maximum_fusion.1
  193.3 35.8 %all-to-all-done.3 = f32[16,2,2,64,128]{4,3,2,1,0:T(8,128)} async-done(((f32[16,2,2,64,128]{4,3,2,1,0:T(8,128)}), f32[16,2,2,64,128]{4,3,2,1,0:T(8,128)}, u32[]{:S(2)}, u32[]{:S(2)}) %all-to-all-start.3) | async-done | bytes 2097184 | tf_op jit(solution)/shard_map/all_to_all | solution.py:135
  229.1 1.7 fusion.88
  231.6 1.1 fusion.36
  233.5 1.1 fusion.34
  234.6 0.9 fusion.46
  235.6 0.7 copy.203
  236.3 0.7 copy.202
  (113 shorter events, 7.4 us)
Async XLA Ops:
  0.6 31.5 %copy-start.12 = (s32[128,2,8]{0,2,1:T(8,128)S(1)}, s32[128,2,8]{0,2,1:T(8,128)}, u32[]{:S(2)}) copy-start(s32[128,2,8]{0,2,1:T(8,128)} %param.9) | copy-start | bytes 24580
  2.2 10.3 %all-to-all-start.1 = ((s32[16,1,2]{2,1,0:T(1,128)}), s32[16,1,2]{2,1,0:T(1,128)S(1)}, u32[]{:S(2)}, u32[]{:S(2)}) async-start(s32[16,1,2]{2,1,0:T(1,128)} %copy.167), calls=%async_computation.1 | async-start | bytes 16384 | tf_op jit(solution)/shard_map/all_to_all | solution.py:76
  8.9 3.6 %copy-start.19 = (pred[16]{0:T(512)(128)(4,1)}, pred[16]{0:T(512)(128)(4,1)S(1)}, u32[]{:S(2)}) copy-start(pred[16]{0:T(512)(128)(4,1)S(1)} %get-tuple-element.113) | copy-start | bytes 52
  9.0 13.5 %copy-start.21 = (pred[16]{0:T(512)(128)(4,1)}, pred[16]{0:T(512)(128)(4,1)S(1)}, u32[]{:S(2)}) copy-start(pred[16]{0:T(512)(128)(4,1)S(1)} %get-tuple-element.112) | copy-start | bytes 52
  9.2 3.3 %copy-start.15 = (s32[16]{0:T(128)}, s32[16]{0:T(128)S(1)}, u32[]{:S(2)}) copy-start(s32[16]{0:T(128)S(1)} %add_reduce_fusion) | copy-start | bytes 196
  9.4 3.1 %copy-start.17 = (s32[16]{0:T(128)}, s32[16]{0:T(128)S(1)}, u32[]{:S(2)}) copy-start(s32[16]{0:T(128)S(1)} %add_reduce_fusion.1) | copy-start | bytes 196
  12.6 9.8 %all-to-all-start = ((s32[16,1,2]{2,1,0:T(1,128)}), s32[16,1,2]{2,1,0:T(1,128)S(1)}, u32[]{:S(2)}, u32[]{:S(2)}) async-start(s32[16,1,2]{2,1,0:T(1,128)} %copy.164), calls=%async_computation | async-start | bytes 16384 | tf_op jit(solution)/shard_map/all_to_all | solution.py:77
  18.6 3.8 %copy-start.13 = (s32[16,1,2]{0,2,1:T(2,128)}, s32[16,1,2]{0,2,1:T(2,128)S(1)}, u32[]{:S(2)}) copy-start(s32[16,1,2]{0,2,1:T(2,128)S(1)} %copy.168) | copy-start | bytes 388
  22.4 0.5 copy-start.25
  24.9 31.8 %all-to-all-start.2 = ((bf16[16,2,2,64,128]{4,3,2,1,0:T(8,128)(2,1)}), bf16[16,2,2,64,128]{4,3,2,1,0:T(8,128)(2,1)}, u32[]{:S(2)}, u32[]{:S(2)}) async-start(bf16[16,2,2,64,128]{4,3,2,1,0:T(8,128)(2,1)} %broadcast_select_fusion.2), calls=%async_computation.2 | async-start | bytes 2097152 | tf_op jit(solution)/shard_map/all_to_all | solution.py:85
  32.7 3.8 %copy-start.3 = (pred[128,576]{1,0:T(8,128)(4,1)}, pred[128,576]{1,0:T(8,128)(4,1)S(1)}, u32[]{:S(2)}) copy-start(pred[128,576]{1,0:T(8,128)(4,1)S(1)} %copy.161) | copy-start | bytes 221188
  33.0 5.7 %copy-start.2 = (bf16[128,32,128]{2,1,0:T(8,128)(2,1)S(1)}, bf16[128,32,128]{2,1,0:T(8,128)(2,1)}, u32[]{:S(2)}) copy-start(bf16[128,32,128]{2,1,0:T(8,128)(2,1)} %param.8) | copy-start | bytes 3145732
  61.7 0.7 copy-start.5
  122.9 5.2 %copy-start.7 = (bf16[128,16,128]{2,1,0:T(8,128)(2,1)S(1)}, bf16[128,16,128]{2,1,0:T(8,128)(2,1)}, u32[]{:S(2)}) copy-start(bf16[128,16,128]{2,1,0:T(8,128)(2,1)} %get-tuple-element.86) | copy-start | bytes 1572868
  128.2 3.8 %copy-start.18 = (s32[16]{0:T(128)S(1)}, s32[16]{0:T(128)}, u32[]{:S(2)}) copy-start(s32[16]{0:T(128)} %copy-done.17) | copy-start | bytes 196
  128.2 3.8 %copy-start.22 = (pred[16]{0:T(512)(128)(4,1)S(1)}, pred[16]{0:T(512)(128)(4,1)}, u32[]{:S(2)}) copy-start(pred[16]{0:T(512)(128)(4,1)} %copy-done.21) | copy-start | bytes 52
  164.2 5.2 %copy-start.6 = (bf16[128,16,128]{2,1,0:T(8,128)(2,1)S(1)}, bf16[128,16,128]{2,1,0:T(8,128)(2,1)}, u32[]{:S(2)}) copy-start(bf16[128,16,128]{2,1,0:T(8,128)(2,1)} %get-tuple-element.87) | copy-start | bytes 1572868
  169.4 4.4 %copy-start.16 = (s32[16]{0:T(128)S(1)}, s32[16]{0:T(128)}, u32[]{:S(2)}) copy-start(s32[16]{0:T(128)} %copy-done.15) | copy-start | bytes 196
  169.4 4.4 %copy-start.20 = (pred[16]{0:T(512)(128)(4,1)S(1)}, pred[16]{0:T(512)(128)(4,1)}, u32[]{:S(2)}) copy-start(pred[16]{0:T(512)(128)(4,1)} %copy-done.19) | copy-start | bytes 52
  169.4 5.0 %copy-start = (f32[16,1,2,64,128]{4,0,3,2,1:T(8,128)S(1)}, f32[16,1,2,64,128]{4,0,3,2,1:T(8,128)}, u32[]{:S(2)}) copy-start(f32[16,1,2,64,128]{4,0,3,2,1:T(8,128)} %convolution_bitcast_fusion.3) | copy-start | bytes 3145732
  173.0 0.8 copy-start.1
  174.6 7.0 %copy-start.14 = (s32[16,1,2]{0,2,1:T(2,128)S(1)}, s32[16,1,2]{0,2,1:T(2,128)}, u32[]{:S(2)}) copy-start(s32[16,1,2]{0,2,1:T(2,128)} %copy-done.13) | copy-start | bytes 388
  174.6 7.0 %copy-start.26 = (s32[16,1,2]{0,2,1:T(2,128)S(1)}, s32[16,1,2]{0,2,1:T(2,128)}, u32[]{:S(2)}) copy-start(s32[16,1,2]{0,2,1:T(2,128)} %copy-done.25) | copy-start | bytes 388
  174.6 7.0 %copy-start.8 = (f32[2048]{0:T(1024)S(1)}, f32[2048]{0:T(1024)}, u32[]{:S(2)}) copy-start(f32[2048]{0:T(1024)} %get-tuple-element.120) | copy-start | bytes 24580
  174.6 7.0 %copy-start.10 = (f32[2048]{0:T(1024)S(1)}, f32[2048]{0:T(1024)}, u32[]{:S(2)}) copy-start(f32[2048]{0:T(1024)} %fusion.1) | copy-start | bytes 24580
  174.7 7.0 %copy-start.23 = (f32[2048]{0:T(1024)S(1)}, f32[2048]{0:T(1024)}, u32[]{:S(2)}) copy-start(f32[2048]{0:T(1024)} %get-tuple-element.122) | copy-start | bytes 24580
  176.6 11.1 %slice-start = ((s8[4718592]{0:T(1024)(128)(4,1)}), s8[524288]{0:T(1024)(128)(4,1)S(1)}, s32[]{:S(2)}) async-start(s8[4718592]{0:T(1024)(128)(4,1)} %bitcast.229), calls=%async_computation.4 | async-start | bytes 1048576
  176.6 52.5 %all-to-all-start.3 = ((f32[16,2,2,64,128]{4,3,2,1,0:T(8,128)}), f32[16,2,2,64,128]{4,3,2,1,0:T(8,128)}, u32[]{:S(2)}, u32[]{:S(2)}) async-start(f32[16,2,2,64,128]{4,3,2,1,0:T(8,128)} %copy.197), calls=%async_computation.3 | async-start | bytes 4194304 | tf_op jit(solution)/shard_map/all_to_all | solution.py:135
  181.6 6.1 %slice-start.1 = ((s8[4718592]{0:T(1024)(128)(4,1)}), s8[4194304]{0:T(1024)(128)(4,1)S(1)}, s32[]{:S(2)}) async-start(s8[4718592]{0:T(1024)(128)(4,1)} %bitcast.229), calls=%async_computation.5 | async-start | bytes 8388608
  181.7 6.1 %copy-start.4 = (bf16[9,1,64,128]{3,2,1,0:T(8,128)(2,1)S(1)}, bf16[9,1,64,128]{3,2,1,0:T(8,128)(2,1)}, u32[]{:S(2)}) copy-start(bf16[9,1,64,128]{3,2,1,0:T(8,128)(2,1)} %get-tuple-element.93) | copy-start | bytes 442372
  181.7 6.1 %copy-start.9 = (f32[2048]{0:T(1024)S(1)}, f32[2048]{0:T(1024)}, u32[]{:S(2)}) copy-start(f32[2048]{0:T(1024)} %get-tuple-element.116) | copy-start | bytes 24580
  181.7 6.1 %copy-start.11 = (f32[2048]{0:T(1024)S(1)}, f32[2048]{0:T(1024)}, u32[]{:S(2)}) copy-start(f32[2048]{0:T(1024)} %fusion.3) | copy-start | bytes 24580
  181.7 6.1 %copy-start.24 = (f32[2048]{0:T(1024)S(1)}, f32[2048]{0:T(1024)}, u32[]{:S(2)}) copy-start(f32[2048]{0:T(1024)} %get-tuple-element.118) | copy-start | bytes 24580
where the time goes:
time: 239 us; the launch traced here: 237 us
  local copies, waits for them, and re-layouts  73.9 us (31%)
  waiting for transfers between devices  56.8 us (24%)
  matrix products  50.2 us (21%)
  other arithmetic  30.5 us (13%)
  starting transfers between devices  24.2 us (10%)
    all_to_all x1, waiting for transfers between devices, local(): lax.all_to_all(outgoing, 'ctx', split_axis=0, concat_axis=0, tiled=True)  35.8 us
    all_to_all x1, waiting for transfers between devices, local(): lax.all_to_all(outgoing_tiles, 'ctx', split_axis=0, concat_axis=0, tiled=...  16.9 us
    dot_general x2, matrix products, visit(): lax.dot_general(upstream_rows, pool_values, contract_last, preferred_elem...  13.7 us
    dot_general x2, other arithmetic, visit(): lax.dot_general(dscore, query_rows, contract_rows, preferred_element_type...  13.4 us
    dot_general x2, local copies, waits for them, and re-layouts, visit(): lax.dot_general(upstream_rows, pool_values, contract_last, preferred_elem...  11.6 us
    mul x2, local copies, waits for them, and re-layouts, visit(): scores = scores.reshape(block_rows, per_group, key_count) * scaling  11.6 us
    dot_general x2, local copies, waits for them, and re-layouts, visit(): lax.dot_general(weights_low, upstream_rows, contract_rows, preferred_elem...  10.5 us
    dot_general x2, matrix products, visit(): jnp.dot(dscore, pool_keys, preferred_element_type=jnp.float32)  10.5 us
  transfers between devices with their start and end apart: 4, of which 4 were waited for; matrix products, arithmetic and copies ran while one was open for 10% of the time, Pallas kernels for 0%

commit v1 on v0

v1 whole, which is shorter than its diff:
```python
import functools
import math

import jax
import jax.numpy as jnp
from jax import lax
from jax.experimental import pallas as pl
from jax.experimental.pallas import tpu as pltpu
from jax.sharding import PartitionSpec as P

BLK = 64
NEG = -1e30
ID_ROWS = 16
LOG2E = math.log2(math.e)
NT = (((1,), (1,)), ((), ()))
NN = (((1,), (0,)), ((), ()))


def barrier_all(n, me):
    barrier = pltpu.get_barrier_semaphore()

    def greet(k, carry):
        peer = lax.rem(me + k, n)
        pl.semaphore_signal(
            barrier, inc=1, device_id={"ctx": peer}, device_id_type=pl.DeviceIdType.MESH
        )
        return carry

    lax.fori_loop(1, n, greet, 0)
    pl.semaphore_wait(barrier, n - 1)


def gather_kernel(n, kv_ref, out_ref, send_sem, fwd_sem, recv_sem, local_sem):
    me = lax.axis_index("ctx")
    sib = me + 1 - 2 * lax.rem(me, 2)
    half = n // 2
    barrier_all(n, me)

    def direct(k):
        return pltpu.make_async_remote_copy(
            src_ref=kv_ref,
            dst_ref=out_ref.at[me],
            send_sem=send_sem.at[k],
            recv_sem=recv_sem.at[me],
            device_id={"ctx": lax.rem(me + 2 * k, n)},
            device_id_type=pl.DeviceIdType.MESH,
        )

    def forward(src):
        return pltpu.make_async_remote_copy(
            src_ref=out_ref.at[src],
            dst_ref=out_ref.at[src],
            send_sem=fwd_sem.at[src],
            recv_sem=recv_sem.at[src],
            device_id={"ctx": sib},
            device_id_type=pl.DeviceIdType.MESH,
        )

    def arrival(src):
        return pltpu.make_async_remote_copy(
            src_ref=kv_ref,
            dst_ref=out_ref.at[src],
            send_sem=send_sem.at[0],
            recv_sem=recv_sem.at[src],
            device_id={"ctx": sib},
            device_id_type=pl.DeviceIdType.MESH,
        )

    to_sib = pltpu.make_async_remote_copy(
        src_ref=kv_ref,
        dst_ref=out_ref.at[me],
        send_sem=send_sem.at[0],
        recv_sem=recv_sem.at[me],
        device_id={"ctx": sib},
        device_id_type=pl.DeviceIdType.MESH,
    )

    @pl.loop(1, half)
    def _(k):
        direct(k).start()

    to_sib.start()
    own = pltpu.make_async_copy(kv_ref, out_ref.at[me], local_sem)
    own.start()

    @pl.loop(1, half)
    def _(k):
        src = lax.rem(me + 2 * (half - k), n)
        arrival(src).wait_recv()
        forward(src).start()

    @pl.loop(0, half)
    def _(k):
        arrival(lax.rem(sib + 2 * k, n)).wait_recv()

    own.wait()
    to_sib.wait_send()

    @pl.loop(1, half)
    def _(k):
        direct(k).wait_send()
        forward(lax.rem(me + 2 * (half - k), n)).wait_send()


def attend(g, per_group, chunk_tokens, picked_ref, q_ref, do_ref, dq_ref, pool_ref, acc_ref):
    tokens, _, dh = q_ref.shape
    own_rows = tokens
    keys = pool_ref.shape[1]
    slots = keys // BLK
    own_slots = own_rows // BLK
    scaling = 1.0 / math.sqrt(dh)
    log_scale = scaling * LOG2E
    rows = chunk_tokens * per_group
    shift = per_group.bit_length() - 1
    pool_k = pool_ref[0]
    pool_v = pool_ref[1]
    pool_kt = pool_k.T
    acc_ref[...] = jnp.zeros_like(acc_ref)
    heads = slice(g * per_group, (g + 1) * per_group)

    @pl.loop(0, tokens // chunk_tokens)
    def _(c):
        t0 = pl.multiple_of(c * chunk_tokens, chunk_tokens)
        q = q_ref[pl.ds(t0, chunk_tokens), heads, :].reshape(rows, dh)
        do = do_ref[pl.ds(t0, chunk_tokens), heads, :].reshape(rows, dh)
        row_tok = t0 + (lax.broadcasted_iota(jnp.int32, (tokens, rows), 1) >> shift)
        tok = lax.broadcasted_iota(jnp.int32, (tokens, rows), 0)
        spread = jnp.where(row_tok == tok, 1.0, 0.0).astype(jnp.bfloat16)
        seen = lax.dot_general(picked_ref[g], spread, NN, preferred_element_type=jnp.float32)
        bias = (seen - 1.0) * (-NEG)
        s = lax.dot_general(pool_k, q, NT, preferred_element_type=jnp.float32)
        dp = lax.dot_general(pool_v, do, NT, preferred_element_type=jnp.float32)
        pieces = []
        for j in range(slots):
            piece = s[j * BLK : (j + 1) * BLK] + bias[j : j + 1]
            if j < own_slots:
                key_pos = j * BLK + lax.broadcasted_iota(jnp.int32, (BLK, rows), 0)
                causal = key_pos <= row_tok[:BLK]
                piece = jnp.where(causal, piece, NEG)
            pieces.append(piece)
        s = jnp.concatenate(pieces, axis=0)
        peak = jnp.max(s, axis=0, keepdims=True)
        e = jnp.exp2((s - peak) * log_scale)
        total = jnp.sum(e, axis=0, keepdims=True)
        weighted = jnp.sum(e * dp, axis=0, keepdims=True)
        inv = 1.0 / total
        inner = weighted * inv
        p = e * inv
        ds = (p * (dp - inner)).astype(jnp.bfloat16)
        p = p.astype(jnp.bfloat16)
        dqt = lax.dot_general(pool_kt, ds, NN, preferred_element_type=jnp.float32)
        dq = (dqt * scaling).T.astype(jnp.bfloat16)
        dq_ref[pl.ds(t0, chunk_tokens), heads, :] = dq.reshape(chunk_tokens, per_group, dh)
        acc_ref[0] += lax.dot_general(ds, q, NN, preferred_element_type=jnp.float32)
        acc_ref[1] += lax.dot_general(p, do, NN, preferred_element_type=jnp.float32)

    acc_ref[0] = acc_ref[0] * scaling


def fill_pool(g, n_far, far_owner, far_block, own_kv, gathered_ref, pool_ref):
    own_rows = own_kv.shape[2]
    pool_ref[:, :own_rows, :] = own_kv[g]
    for s in range(n_far):
        owner = far_owner[g, s]
        start = pl.multiple_of(far_block[g, s] * BLK, BLK)
        lo = own_rows + s * BLK
        for kv in range(2):
            pool_ref[kv, lo : lo + BLK, :] = gathered_ref[owner, g, kv, pl.ds(start, BLK), :]


def fill_outbox(g, n, own_rows, slot_of, live, block_of, acc_ref, outbox):
    def fill(j, carry):
        start = pl.multiple_of(own_rows + slot_of[g, j] * BLK, BLK)
        keep = live[g, j].astype(jnp.float32)
        base = ID_ROWS + g * 2 * BLK
        for kv in range(2):
            part = acc_ref[kv, pl.ds(start, BLK), :] * keep
            outbox[j, base + kv * BLK : base + (kv + 1) * BLK, :] = part.astype(jnp.bfloat16)
        return carry

    lax.fori_loop(0, n, fill, 0)


def fill_ids(n, groups, block_of, outbox):
    dh = outbox.shape[2]

    def fill(j, carry):
        row = lax.broadcasted_iota(jnp.int32, (ID_ROWS, dh), 0)
        ids = jnp.zeros((ID_ROWS, dh), jnp.float32)
        for g in range(groups):
            ids = jnp.where(row == g, block_of[g, j].astype(jnp.float32), ids)
        outbox[j, :ID_ROWS, :] = ids.astype(jnp.bfloat16)
        return carry

    lax.fori_loop(0, n, fill, 0)


def attend_kernel(
    n, n_far, chunk_tokens,
    far_owner, far_block, slot_of, live, block_of,
    picked_ref, q_ref, do_ref, own_kv, gathered_ref,
    dq_ref, outbox, own_grad, pool_ref, acc_ref,
):
    groups = own_kv.shape[0]
    per_group = q_ref.shape[1] // groups
    own_rows = q_ref.shape[0]
    fill_ids(n, groups, block_of, outbox)
    for g in range(groups):
        fill_pool(g, n_far, far_owner, far_block, own_kv, gathered_ref, pool_ref)
        attend(g, per_group, chunk_tokens, picked_ref, q_ref, do_ref, dq_ref, pool_ref, acc_ref)
        own_grad[g] = acc_ref[:, :own_rows, :]
        fill_outbox(g, n, own_rows, slot_of, live, block_of, acc_ref, outbox)


def reduce_group(g, n, me, inbox, own_grad, out_ref):
    own_blocks = own_grad.shape[2] // BLK
    dh = own_grad.shape[3]
    base = ID_ROWS + g * 2 * BLK

    def add(k, sums):
        src = lax.rem(me + k, n)
        which = inbox[src, :ID_ROWS, :].astype(jnp.float32)[g : g + 1]
        out = []
        for kv in range(2):
            part = inbox[src, base + kv * BLK : base + (kv + 1) * BLK, :].astype(jnp.float32)
            for b in range(own_blocks):
                out.append(sums[kv * own_blocks + b] + jnp.where(which == float(b), part, 0.0))
        return tuple(out)

    first = tuple(
        own_grad[g, kv, b * BLK : (b + 1) * BLK, :] for kv in range(2) for b in range(own_blocks)
    )
    sums = lax.fori_loop(1, n, add, first)
    for kv in range(2):
        for b in range(own_blocks):
            out_ref[g, kv, b * BLK : (b + 1) * BLK, :] = sums[kv * own_blocks + b].astype(
                jnp.bfloat16
            )


def return_kernel(n, outbox, own_grad, out_ref, inbox, send_sem, recv_sem):
    me = lax.axis_index("ctx")
    barrier_all(n, me)

    def send(k):
        peer = lax.rem(me + k, n)
        return pltpu.make_async_remote_copy(
            src_ref=outbox.at[peer],
            dst_ref=inbox.at[me],
            send_sem=send_sem.at[peer],
            recv_sem=recv_sem.at[me],
            device_id={"ctx": peer},
            device_id_type=pl.DeviceIdType.MESH,
        )

    def arrival(src):
        return pltpu.make_async_remote_copy(
            src_ref=outbox.at[src],
            dst_ref=inbox.at[src],
            send_sem=send_sem.at[src],
            recv_sem=recv_sem.at[src],
            device_id={"ctx": src},
            device_id_type=pl.DeviceIdType.MESH,
        )

    @pl.loop(1, n)
    def _(k):
        send(k).start()

    @pl.loop(1, n)
    def _(k):
        arrival(lax.rem(me + n - k, n)).wait_recv()

    for g in range(own_grad.shape[0]):
        reduce_group(g, n, me, inbox, own_grad, out_ref)

    @pl.loop(1, n)
    def _(k):
        send(k).wait_send()


def tables(selected, tokens, n, fetched):
    own_blocks = tokens // BLK
    me = lax.axis_index("ctx")
    peers = jnp.arange(n, dtype=jnp.int32)
    owner_of = selected // own_blocks
    local_of = selected - owner_of * own_blocks
    match = (owner_of[..., None] == peers) & (peers != me)
    code = jnp.max(jnp.where(match, local_of[..., None] + 1, 0), axis=(0, 2))
    live = (code > 0).astype(jnp.int32)
    block_of = jnp.maximum(code - 1, 0)
    before = (peers[None, :] < peers[:, None]).astype(jnp.int32)
    slot = jnp.sum(before[None] * live[:, None, :], axis=2)
    slot_of = jnp.minimum(slot, fetched - 1)
    pick = (slot[:, None, :] == jnp.arange(fetched)[None, :, None]) & (live[:, None, :] > 0)
    far_owner = jnp.sum(jnp.where(pick, peers, 0), axis=2)
    far_block = jnp.sum(jnp.where(pick, block_of[:, None, :], 0), axis=2)
    far_live = jnp.any(pick, axis=2)
    groups = selected.shape[1]
    own_ids = me * own_blocks + jnp.arange(own_blocks, dtype=jnp.int32)
    far_ids = jnp.where(far_live, far_owner * own_blocks + far_block, -1)
    pool = jnp.concatenate(
        [jnp.broadcast_to(own_ids, (groups, own_blocks)), far_ids], axis=1
    )
    pad = -pool.shape[1] % 16
    pool = jnp.pad(pool, ((0, 0), (0, pad)), constant_values=-1)
    now = me * own_blocks + jnp.arange(tokens, dtype=jnp.int32) // BLK
    chosen = selected.transpose(1, 2, 0)
    picked = jnp.any(chosen[:, None] == pool[:, :, None, None], axis=2)
    picked = picked & (pool[:, :, None] <= now)
    return far_owner, far_block, slot_of, live, block_of, picked.astype(jnp.bfloat16)


def local(queries, keys, values, grad_out, selected):
    tokens, head_count, dh = queries.shape
    groups = keys.shape[1]
    own_blocks = tokens // BLK
    n = lax.axis_size("ctx")
    fetched = min(n - 2, max(selected.shape[2] - own_blocks, 4)) + 1
    pool_rows = (own_blocks + fetched) * BLK
    msg = ID_ROWS + groups * 2 * BLK
    far_owner, far_block, slot_of, live, block_of, picked = tables(selected, tokens, n, fetched)
    own_kv = jnp.stack([keys, values], axis=0).transpose(2, 0, 1, 3)
    any_spec = pl.BlockSpec(memory_space=pl.ANY)
    vmem = pl.BlockSpec(memory_space=pltpu.VMEM)
    smem = pl.BlockSpec(memory_space=pltpu.SMEM)
    gathered = pl.pallas_call(
        functools.partial(gather_kernel, n),
        out_shape=jax.ShapeDtypeStruct((n,) + own_kv.shape, jnp.bfloat16),
        in_specs=[vmem],
        out_specs=vmem,
        scratch_shapes=[
            pltpu.SemaphoreType.DMA((n,)),
            pltpu.SemaphoreType.DMA((n,)),
            pltpu.SemaphoreType.DMA((n,)),
            pltpu.SemaphoreType.DMA,
        ],
        compiler_params=pltpu.CompilerParams(collective_id=0, has_side_effects=True),
    )(own_kv)
    dq, outbox, own_grad = pl.pallas_call(
        functools.partial(attend_kernel, n, fetched, min(tokens, 32)),
        out_shape=(
            jax.ShapeDtypeStruct(queries.shape, jnp.bfloat16),
            jax.ShapeDtypeStruct((n, msg, dh), jnp.bfloat16),
            jax.ShapeDtypeStruct((groups, 2, tokens, dh), jnp.float32),
        ),
        in_specs=[smem] * 5 + [vmem] * 5,
        out_specs=(vmem, vmem, vmem),
        scratch_shapes=[
            pltpu.VMEM((2, pool_rows, dh), jnp.bfloat16),
            pltpu.VMEM((2, pool_rows, dh), jnp.float32),
        ],
    )(far_owner, far_block, slot_of, live, block_of, picked, queries, grad_out, own_kv, gathered)
    summed = pl.pallas_call(
        functools.partial(return_kernel, n),
        out_shape=jax.ShapeDtypeStruct((groups, 2, tokens, dh), jnp.bfloat16),
        in_specs=[vmem, vmem],
        out_specs=vmem,
        scratch_shapes=[
            pltpu.VMEM((n, msg, dh), jnp.bfloat16),
            pltpu.SemaphoreType.DMA((n,)),
            pltpu.SemaphoreType.DMA((n,)),
        ],
        compiler_params=pltpu.CompilerParams(collective_id=1, has_side_effects=True),
    )(outbox, own_grad)
    key_grad = summed[:, 0].transpose(1, 0, 2)
    value_grad = summed[:, 1].transpose(1, 0, 2)
    return dq, key_grad, value_grad


def solution(mesh):
    spec = P(("rep", "ctx"), None, None)
    return jax.shard_map(
        local, mesh=mesh, in_specs=(spec,) * 5, out_specs=(spec,) * 3, check_vma=False
    )
```

time: 239 us -> 88.1 us (0.37)
  the two profiles are of different devices: /device:TPU:15 before, /device:TPU:13 now
where the time goes in v1:
time: 88.1 us; the launch traced here: 87.8 us
  Pallas kernels  79.2 us (90%)
  other arithmetic  4.17 us (5%)
  local copies, waits for them, and re-layouts  3.59 us (4%)
    pallas_call x1, Pallas kernels, local(): pl.pallas_call(functools.partial(gather_kernel, n), out_shape=jax.ShapeDt...  31.8 us
    pallas_call x1, Pallas kernels, local(): pl.pallas_call(functools.partial(return_kernel, n), out_shape=jax.ShapeDt...  31.6 us
    pallas_call x1, Pallas kernels, local(): pl.pallas_call(functools.partial(attend_kernel, n, fetched, min(tokens, 3...  15.8 us

profile of v1, /device:TPU:13, one launch (start us, length us, event | category | flops | bytes accessed | tf_op | source)
XLA Modules:
  0.0 87.8 jit_solution(1148664295281349393)
XLA Ops:
  0.7 0.7 add_select_fusion
  1.4 0.2 select_reduce_fusion
  1.6 0.0 copy-start
  1.6 0.1 multiply_reduce_fusion
  1.8 0.2 fusion.5
  1.9 0.1 copy.27
  2.0 0.6 add_maximum_fusion
  2.6 0.0 copy-start.3
  2.6 0.1 select_reduce_fusion.1
  2.7 0.0 copy-start.1
  2.7 0.0 copy-start.2
  2.8 0.1 copy.36
  2.8 0.1 copy.35
  3.0 0.1 copy.28
  3.0 0.1 pad_add_fusion
  3.1 0.8 compare_reduce_fusion
  4.0 0.7 and_convert_fusion.picked_ref
  4.6 0.9 %copy_bitcast_fusion = (bf16[1,128,2,128]{3,1,0,2:T(8,128)(2,1)S(1)}, bf16[1,128,2,128]{3,1,0,2:T(8,128)(2,1)S(1)}) fusion(bf16[128,2,128]{2,1,0:T(2,128)(2,1)} %param.7, bf16[128,2,128]{2,1,0:T(2,128)(2,1)} %param.6), kind=kLoop, calls=%fused_computation.5 | loop fusion | bytes 262144 | tf_op jit(solution)/shard_map/stack | solution.py:323
  5.5 0.7 maximum_bitcast_fusion.kv_ref.own_kv
  6.2 31.8 %shard_map.76.gathered_ref = bf16[16,2,2,128,128]{4,3,2,1,0:T(8,128)(2,1)} custom-call(bf16[2,2,128,128]{3,2,1,0:T(8,128)(2,1)} %maximum_bitcast_fusion.kv_ref.own_kv), custom_call_target="tpu_custom_call" | custom-call | tf_op jit(solution)/shard_map/pallas_call | solution.py:327
  38.0 0.0 copy-done
  38.0 0.0 copy-done.3
  38.0 0.0 copy-done.1
  38.1 0.0 copy-done.2
  38.1 15.8 %shard_map.77 = (bf16[128,32,128]{2,1,0:T(8,128)(2,1)}, bf16[16,272,128]{2,1,0:T(8,128)(2,1)}, f32[2,2,128,128]{3,2,1,0:T(8,128)}) custom-call(s32[2,7]{1,0:T(2,128)} %copy-done.2, s32[2,7]{1,0:T(2,128)} %copy-done.1, s32[2,16]{1,0:T(2,128)} %get-tuple-element.29.slot_of, s32[2,16]{1,0:T(2,128)} %copy-done, s32[2,16]{1,0:T(2,128)} %copy-done.3, ...), custom_call_target="tpu_custom_call" | custom-call | tf_op jit(solution)/shard_map/pallas_call | solution.py:340
  53.9 31.6 %shard_map.78 = bf16[2,2,128,128]{3,2,1,0:T(8,128)(2,1)} custom-call(bf16[16,272,128]{2,1,0:T(8,128)(2,1)} %get-tuple-element.7.outbox, f32[2,2,128,128]{3,2,1,0:T(8,128)} %get-tuple-element.8.own_grad), custom_call_target="tpu_custom_call" | custom-call | tf_op jit(solution)/shard_map/pallas_call | solution.py:354
  85.5 0.9 %slice_bitcast_fusion = (bf16[128,2,128]{2,0,1:T(8,128)(2,1)S(1)}, bf16[128,2,128]{2,0,1:T(8,128)(2,1)S(1)}) fusion(bf16[2,2,128,128]{3,2,1,0:T(8,128)(2,1)} %shard_map.78), kind=kLoop, calls=%fused_computation.7 | loop fusion | bytes 262144 | tf_op jit(solution)/shard_map/transpose | solution.py:367
  86.4 0.7 copy.34
  87.1 0.7 copy.33
  (8 shorter events, 0.1 us)
Async XLA Ops:
  1.6 36.4 %copy-start = (s32[2,16]{1,0:T(2,128)}, s32[2,16]{1,0:T(2,128)S(1)}, u32[]{:S(2)}) copy-start(s32[2,16]{1,0:T(2,128)S(1)} %get-tuple-element.25.live) | copy-start | bytes 388
  2.6 35.4 %copy-start.3 = (s32[2,16]{1,0:T(2,128)}, s32[2,16]{1,0:T(2,128)S(1)}, u32[]{:S(2)}) copy-start(s32[2,16]{1,0:T(2,128)S(1)} %get-tuple-element.28.block_of) | copy-start | bytes 388
  2.7 35.3 %copy-start.1 = (s32[2,7]{1,0:T(2,128)}, s32[2,7]{1,0:T(2,128)S(1)}, u32[]{:S(2)}) copy-start(s32[2,7]{1,0:T(2,128)S(1)} %get-tuple-element.18.far_block) | copy-start | bytes 172
  2.7 35.3 %copy-start.2 = (s32[2,7]{1,0:T(2,128)}, s32[2,7]{1,0:T(2,128)S(1)}, u32[]{:S(2)}) copy-start(s32[2,7]{1,0:T(2,128)S(1)} %get-tuple-element.19.far_owner) | copy-start | bytes 172

commit v2 on v1

v2 whole, which is shorter than its diff:
```python
import functools
import math

import jax
import jax.numpy as jnp
from jax import lax
from jax.experimental import pallas as pl
from jax.experimental.pallas import tpu as pltpu
from jax.sharding import PartitionSpec as P

BLK = 64
NEG = -1e30
ID_ROWS = 16
LOG2E = math.log2(math.e)
NT = (((1,), (1,)), ((), ()))
NN = (((1,), (0,)), ((), ()))


def barrier_all(n, me):
    barrier = pltpu.get_barrier_semaphore()

    def greet(k, carry):
        peer = lax.rem(me + k, n)
        pl.semaphore_signal(
            barrier, inc=1, device_id={"ctx": peer}, device_id_type=pl.DeviceIdType.MESH
        )
        return carry

    lax.fori_loop(1, n, greet, 0)
    pl.semaphore_wait(barrier, n - 1)


def attend(
    g, per_group, chunk_tokens, lo, hi, picked_ref, q_ref, do_ref, dq_ref, pool_ref, acc_ref
):
    tokens, _, dh = q_ref.shape
    own_rows = tokens
    keys = pool_ref.shape[1]
    slots = keys // BLK
    own_slots = own_rows // BLK
    scaling = 1.0 / math.sqrt(dh)
    log_scale = scaling * LOG2E
    rows = chunk_tokens * per_group
    shift = per_group.bit_length() - 1
    pool_k = pool_ref[0]
    pool_v = pool_ref[1]
    pool_kt = pool_k.T
    heads = slice(g * per_group, (g + 1) * per_group)

    @pl.loop(lo, hi)
    def _(c):
        t0 = pl.multiple_of(c * chunk_tokens, chunk_tokens)
        q = q_ref[pl.ds(t0, chunk_tokens), heads, :].reshape(rows, dh)
        do = do_ref[pl.ds(t0, chunk_tokens), heads, :].reshape(rows, dh)
        row_tok = t0 + (lax.broadcasted_iota(jnp.int32, (tokens, rows), 1) >> shift)
        tok = lax.broadcasted_iota(jnp.int32, (tokens, rows), 0)
        spread = jnp.where(row_tok == tok, 1.0, 0.0).astype(jnp.bfloat16)
        seen = lax.dot_general(picked_ref[g], spread, NN, preferred_element_type=jnp.float32)
        bias = (seen - 1.0) * (-NEG)
        s = lax.dot_general(pool_k, q, NT, preferred_element_type=jnp.float32)
        dp = lax.dot_general(pool_v, do, NT, preferred_element_type=jnp.float32)
        pieces = []
        for j in range(slots):
            piece = s[j * BLK : (j + 1) * BLK] + bias[j : j + 1]
            if j < own_slots:
                key_pos = j * BLK + lax.broadcasted_iota(jnp.int32, (BLK, rows), 0)
                causal = key_pos <= row_tok[:BLK]
                piece = jnp.where(causal, piece, NEG)
            pieces.append(piece)
        s = jnp.concatenate(pieces, axis=0)
        peak = jnp.max(s, axis=0, keepdims=True)
        e = jnp.exp2((s - peak) * log_scale)
        total = jnp.sum(e, axis=0, keepdims=True)
        weighted = jnp.sum(e * dp, axis=0, keepdims=True)
        inv = 1.0 / total
        inner = weighted * inv
        p = e * inv
        ds = (p * (dp - inner)).astype(jnp.bfloat16)
        p = p.astype(jnp.bfloat16)
        dqt = lax.dot_general(pool_kt, ds, NN, preferred_element_type=jnp.float32)
        dq = (dqt * scaling).T.astype(jnp.bfloat16)
        dq_ref[pl.ds(t0, chunk_tokens), heads, :] = dq.reshape(chunk_tokens, per_group, dh)
        dk = lax.dot_general(ds, q, NN, preferred_element_type=jnp.float32)
        dv = lax.dot_general(p, do, NN, preferred_element_type=jnp.float32)
        acc_ref[0] += dk.reshape(slots, BLK, dh)
        acc_ref[1] += dv.reshape(slots, BLK, dh)


def fill_pool(g, n_far, far_owner, far_block, own_kv, gathered_ref, pool_ref):
    own_rows = own_kv.shape[2] * BLK
    pool_ref[:, :own_rows, :] = own_kv[g].reshape(2, own_rows, own_kv.shape[4])
    for s in range(n_far):
        owner = far_owner[g, s]
        block = far_block[g, s]
        lo = own_rows + s * BLK
        for kv in range(2):
            pool_ref[kv, lo : lo + BLK, :] = gathered_ref[owner, kv, block]


def fused_kernel(
    n, cols, n_far, chunk_tokens, groups,
    far_owner, far_block, slot_of, live, block_of,
    picked_ref, q_ref, do_ref, own_kv, dq_ref, out_ref, *scratch,
):
    per_bank = 9
    banks = [scratch[g * per_bank : (g + 1) * per_bank] for g in range(groups)]
    (
        pool_ref, mid_ref, col_send, y_send, sib_send, recv_sem,
        rs_sem, ry_send, ry_recv, rz_send, rz_recv,
    ) = scratch[groups * per_bank :]
    depth = n // (2 * cols)
    chips = n // 2
    me = lax.axis_index("ctx")
    core = lax.rem(me, 2)
    chip = me // 2
    y = lax.rem(chip, cols)
    z = chip // cols
    sib = 2 * chip + 1 - core
    other_y = cols - 1 - y
    y_peer = 2 * (z * cols + other_y) + core
    own_blocks = own_kv.shape[2]
    dh = own_kv.shape[4]
    per_group = q_ref.shape[1] // groups
    chunks = q_ref.shape[0] // chunk_tokens
    scaling = 1.0 / math.sqrt(dh)

    def device(zz, yy, cc):
        return 2 * (zz * cols + yy) + cc

    def remote(src, dst, send, recv, peer):
        return pltpu.make_async_remote_copy(
            src_ref=src,
            dst_ref=dst,
            send_sem=send,
            recv_sem=recv,
            device_id={"ctx": peer},
            device_id_type=pl.DeviceIdType.MESH,
        )

    def col_copy(g, k):
        peer = device(lax.rem(z + k, depth), y, core)
        return remote(
            own_kv.at[g], banks[g][0].at[me], col_send.at[g, k], recv_sem.at[g, me], peer
        )

    def own_copy(g, sem, peer):
        return remote(own_kv.at[g], banks[g][0].at[me], sem, recv_sem.at[g, me], peer)

    def pass_on(g, src, sem, peer):
        slot = banks[g][0].at[src]
        return remote(slot, slot, sem, recv_sem.at[g, src], peer)

    def await_piece(g, src):
        pass_on(g, src, sib_send.at[g, src], sib).wait_recv()

    def gather_start(g):
        if cols > 1:
            own_copy(g, y_send.at[g, z], y_peer).start()

        @pl.loop(1, depth)
        def _(k):
            col_copy(g, k).start()

        own_copy(g, sib_send.at[g, me], sib).start()

    def gather_column(g):
        @pl.loop(1, depth)
        def _(k):
            from_z = lax.rem(z + depth - k, depth)
            src = device(from_z, y, core)
            await_piece(g, src)
            if cols > 1:
                pass_on(g, src, y_send.at[g, from_z], y_peer).start()
            pass_on(g, src, sib_send.at[g, src], sib).start()

    def gather_across(g):
        if cols > 1:
            @pl.loop(0, depth)
            def _(k):
                src = device(lax.rem(z + depth - k, depth), other_y, core)
                await_piece(g, src)
                pass_on(g, src, sib_send.at[g, src], sib).start()

    def gather_end(g):
        @pl.loop(0, chips)
        def _(q):
            await_piece(g, 2 * q + 1 - core)

    def gather_drain(g):
        @pl.loop(1, depth)
        def _(k):
            col_copy(g, k).wait_send()

        if cols > 1:
            @pl.loop(0, depth)
            def _(k):
                pass_on(g, device(k, y, core), y_send.at[g, k], y_peer).wait_send()

        @pl.loop(0, chips)
        def _(q):
            src = 2 * q + core
            pass_on(g, src, sib_send.at[g, src], sib).wait_send()

    def sib_copy(g):
        return remote(banks[g][2], banks[g][3], rs_sem.at[g, 0], rs_sem.at[g, 1], sib)

    def y_copy(g, k):
        return remote(
            banks[g][4].at[k], banks[g][5].at[k], ry_send.at[g, k], ry_recv.at[g, k], y_peer
        )

    def z_copy(g, to_z):
        peer = device(to_z, y, core)
        return remote(
            banks[g][6].at[to_z], banks[g][7].at[z], rz_send.at[g, to_z], rz_recv.at[g, z], peer
        )

    def z_arrival(g, from_z):
        peer = device(from_z, y, core)
        return remote(
            banks[g][6].at[from_z], banks[g][7].at[from_z],
            rz_send.at[g, from_z], rz_recv.at[g, from_z], peer,
        )

    def far_part(g, dest, kv):
        return banks[g][1][kv, own_blocks + slot_of[g, dest]]

    def return_start(g):
        acc_ref, box = banks[g][1], banks[g][2]
        acc_ref[0] = acc_ref[0] * scaling

        @pl.loop(0, chips)
        def _(q):
            dest = 2 * q + 1 - core
            keep = live[g, dest].astype(jnp.float32)
            ids = jnp.full((ID_ROWS, dh), block_of[g, dest].astype(jnp.float32), jnp.float32)
            box[q, :ID_ROWS, :] = ids.astype(jnp.bfloat16)
            for kv in range(2):
                lo = ID_ROWS + kv * BLK
                box[q, lo : lo + BLK, :] = (far_part(g, dest, kv) * keep).astype(jnp.bfloat16)

        sib_copy(g).start()

    def merged(g, zz, yy):
        q = zz * cols + yy
        dest = 2 * q + core
        box = banks[g][3]
        which = box[q, :ID_ROWS, :].astype(jnp.float32)[:1]
        keep = live[g, dest].astype(jnp.float32)
        block = jnp.full((1, dh), block_of[g, dest].astype(jnp.float32), jnp.float32)
        for kv in range(2):
            lo = ID_ROWS + kv * BLK
            theirs = box[q, lo : lo + BLK, :].astype(jnp.float32)
            mine = far_part(g, dest, kv) * keep
            for b in range(own_blocks):
                yield kv, b, (
                    jnp.where(block == float(b), mine, 0.0)
                    + jnp.where(which == float(b), theirs, 0.0)
                )

    def return_across(g):
        sib_copy(g).wait_recv()
        if cols > 1:
            @pl.loop(0, depth)
            def _(k):
                zz = lax.rem(z + 1 + k, depth)
                for kv, b, part in merged(g, zz, other_y):
                    banks[g][4][zz, kv, b] = part.astype(jnp.bfloat16)
                y_copy(g, zz).start()

        @pl.loop(0, depth)
        def _(k):
            for kv, b, part in merged(g, k, y):
                mid_ref[k, kv, b] = part

    def return_column(g):
        @pl.loop(1, depth)
        def _(k):
            to_z = lax.rem(z + k, depth)
            total = mid_ref[to_z]
            if cols > 1:
                y_copy(g, to_z).wait_recv()
                total = total + banks[g][5][to_z].astype(jnp.float32)
            banks[g][6][to_z] = total.astype(jnp.bfloat16)
            z_copy(g, to_z).start()

        total = mid_ref[z] + banks[g][1][:, :own_blocks]
        if cols > 1:
            y_copy(g, z).wait_recv()
            total = total + banks[g][5][z].astype(jnp.float32)
        banks[g][8][...] = total

    def return_end(g):
        @pl.loop(1, depth)
        def _(k):
            from_z = lax.rem(z + depth - k, depth)
            z_arrival(g, from_z).wait_recv()
            banks[g][8][...] += banks[g][7][from_z].astype(jnp.float32)

        out_ref[g] = banks[g][8][...].astype(jnp.bfloat16)

    def return_drain(g):
        sib_copy(g).wait_send()
        if cols > 1:
            @pl.loop(0, depth)
            def _(k):
                y_copy(g, k).wait_send()

        @pl.loop(1, depth)
        def _(k):
            z_copy(g, lax.rem(z + k, depth)).wait_send()

    barrier_all(n, me)
    for g in range(groups):
        gather_start(g)
    for g in range(groups):
        banks[g][1][...] = jnp.zeros_like(banks[g][1])
    gather_column(0)
    gather_across(0)
    gather_end(0)
    for g in range(groups):
        first, last = [], []
        if g + 1 < groups:
            first.append(functools.partial(gather_column, g + 1))
            last.append(functools.partial(gather_across, g + 1))
        if g > 0:
            first.append(functools.partial(return_across, g - 1))
            last.append(functools.partial(return_column, g - 1))
        fill_pool(g, n_far, far_owner, far_block, own_kv, banks[g][0], pool_ref)
        cuts = sorted({0, min(1, chunks), chunks // 2, chunks})
        for i in range(len(cuts) - 1):
            attend(
                g, per_group, chunk_tokens, cuts[i], cuts[i + 1],
                picked_ref, q_ref, do_ref, dq_ref, pool_ref, banks[g][1],
            )
            for step in (first if i == 0 else last if i == len(cuts) - 2 else []):
                step()
        if g + 1 < groups:
            gather_end(g + 1)
        return_start(g)
    final = groups - 1
    return_across(final)
    return_column(final)
    for g in range(groups):
        return_end(g)
    for g in range(groups):
        gather_drain(g)
        return_drain(g)


def columns_of(mesh, n):
    spots = [getattr(d, "coords", None) for d in mesh.devices.reshape(-1, n)[0]]
    if None in spots or n % 2:
        return 1
    cols = sum(spot[2] == spots[0][2] for spot in spots) // 2
    return 2 if cols == 2 and n % 4 == 0 else 1


def tables(selected, tokens, n, fetched):
    own_blocks = tokens // BLK
    me = lax.axis_index("ctx")
    peers = jnp.arange(n, dtype=jnp.int32)
    owner_of = selected // own_blocks
    local_of = selected - owner_of * own_blocks
    match = (owner_of[..., None] == peers) & (peers != me)
    code = jnp.max(jnp.where(match, local_of[..., None] + 1, 0), axis=(0, 2))
    live = (code > 0).astype(jnp.int32)
    block_of = jnp.maximum(code - 1, 0)
    before = (peers[None, :] < peers[:, None]).astype(jnp.int32)
    slot = jnp.sum(before[None] * live[:, None, :], axis=2)
    slot_of = jnp.minimum(slot, fetched - 1)
    pick = (slot[:, None, :] == jnp.arange(fetched)[None, :, None]) & (live[:, None, :] > 0)
    far_owner = jnp.sum(jnp.where(pick, peers, 0), axis=2)
    far_block = jnp.sum(jnp.where(pick, block_of[:, None, :], 0), axis=2)
    far_live = jnp.any(pick, axis=2)
    groups = selected.shape[1]
    own_ids = me * own_blocks + jnp.arange(own_blocks, dtype=jnp.int32)
    far_ids = jnp.where(far_live, far_owner * own_blocks + far_block, -1)
    pool = jnp.concatenate(
        [jnp.broadcast_to(own_ids, (groups, own_blocks)), far_ids], axis=1
    )
    pad = -pool.shape[1] % 16
    pool = jnp.pad(pool, ((0, 0), (0, pad)), constant_values=-1)
    now = me * own_blocks + jnp.arange(tokens, dtype=jnp.int32) // BLK
    chosen = selected.transpose(1, 2, 0)
    picked = jnp.any(chosen[:, None] == pool[:, :, None, None], axis=2)
    picked = picked & (pool[:, :, None] <= now)
    return far_owner, far_block, slot_of, live, block_of, picked.astype(jnp.bfloat16)


def local(cols, queries, keys, values, grad_out, selected):
    tokens, head_count, dh = queries.shape
    groups = keys.shape[1]
    own_blocks = tokens // BLK
    n = lax.axis_size("ctx")
    depth = n // (2 * cols)
    fetched = min(n - 2, max(selected.shape[2] - own_blocks, 4)) + 1
    pool_rows = (own_blocks + fetched) * BLK
    far_owner, far_block, slot_of, live, block_of, picked = tables(selected, tokens, n, fetched)
    own_kv = jnp.stack([keys, values], axis=0).transpose(2, 0, 1, 3)
    piece = (2, own_blocks, BLK, dh)
    own_kv = own_kv.reshape((groups,) + piece)
    vmem = pl.BlockSpec(memory_space=pltpu.VMEM)
    smem = pl.BlockSpec(memory_space=pltpu.SMEM)
    bank = [
        pltpu.VMEM((n,) + piece, jnp.bfloat16),
        pltpu.VMEM((2, pool_rows // BLK, BLK, dh), jnp.float32),
        pltpu.VMEM((n // 2, ID_ROWS + 2 * BLK, dh), jnp.bfloat16),
        pltpu.VMEM((n // 2, ID_ROWS + 2 * BLK, dh), jnp.bfloat16),
        pltpu.VMEM((depth,) + piece, jnp.bfloat16),
        pltpu.VMEM((depth,) + piece, jnp.bfloat16),
        pltpu.VMEM((depth,) + piece, jnp.bfloat16),
        pltpu.VMEM((depth,) + piece, jnp.bfloat16),
        pltpu.VMEM(piece, jnp.float32),
    ]
    dma = pltpu.SemaphoreType.DMA
    dq, summed = pl.pallas_call(
        functools.partial(fused_kernel, n, cols, fetched, min(tokens, 32), groups),
        out_shape=(
            jax.ShapeDtypeStruct(queries.shape, jnp.bfloat16),
            jax.ShapeDtypeStruct((groups,) + piece, jnp.bfloat16),
        ),
        in_specs=[smem] * 5 + [vmem] * 4,
        out_specs=(vmem, vmem),
        scratch_shapes=bank * groups + [
            pltpu.VMEM((2, pool_rows, dh), jnp.bfloat16),
            pltpu.VMEM((depth,) + piece, jnp.float32),
            dma((groups, depth)),
            dma((groups, depth)),
            dma((groups, n)),
            dma((groups, n)),
            dma((groups, 2)),
            dma((groups, depth)),
            dma((groups, depth)),
            dma((groups, depth)),
            dma((groups, depth)),
        ],
        compiler_params=pltpu.CompilerParams(collective_id=0, has_side_effects=True),
    )(far_owner, far_block, slot_of, live, block_of, picked, queries, grad_out, own_kv)
    summed = summed.reshape(groups, 2, tokens, dh)
    key_grad = summed[:, 0].transpose(1, 0, 2)
    value_grad = summed[:, 1].transpose(1, 0, 2)
    return dq, key_grad, value_grad


def solution(mesh):
    spec = P(("rep", "ctx"), None, None)
    cols = columns_of(mesh, mesh.shape["ctx"])
    return jax.shard_map(
        functools.partial(local, cols),
        mesh=mesh,
        in_specs=(spec,) * 5,
        out_specs=(spec,) * 3,
        check_vma=False,
    )
```

time: 88.1 us -> 63.7 us (0.72)
  the two profiles are of different devices: /device:TPU:13 before, /device:TPU:0 now
where the time goes in v2:
time: 63.7 us; the launch traced here: 63.4 us
  Pallas kernels  52.5 us (82%)
  local copies, waits for them, and re-layouts  7.82 us (12%)
  other arithmetic  2.29 us (4%)
  between operations  0.75 us (1%)
    pallas_call x1, Pallas kernels, local(): pl.pallas_call(functools.partial(fused_kernel, n, cols, fetched, min(toke...  52.5 us
    unnamed x19, local copies, waits for them, and re-layouts  6.04 us

profile of v2, /device:TPU:0, one launch (start us, length us, event | category | flops | bytes accessed | tf_op | source)
XLA Modules:
  0.0 63.4 jit_solution(7878880136518855176)
XLA Ops:
  0.6 0.0 copy-start.2
  0.7 0.6 %copy-done.2 = s32[128,2,8]{0,2,1:T(8,128)S(1)} copy-done((s32[128,2,8]{0,2,1:T(8,128)S(1)}, s32[128,2,8]{0,2,1:T(8,128)}, u32[]{:S(2)}) %copy-start.2) | copy-done | bytes 8216
  1.3 0.0 copy-start.1
  1.4 0.0 copy-start
  1.4 0.2 select_reduce_fusion
  1.6 0.0 copy-start.3
  1.6 0.1 multiply_reduce_fusion
  1.7 0.4 copy-done.3
  2.1 0.1 fusion.5
  2.3 0.1 copy.25
  2.4 0.6 add_maximum_fusion
  3.0 0.0 copy-start.6
  3.0 0.6 copy-done.6
  3.5 0.1 select_reduce_fusion.1
  3.7 0.0 copy-start.4
  3.7 0.0 copy-start.5
  3.7 0.6 copy-done.4
  4.3 0.1 copy.33
  4.3 0.0 copy-done.5
  4.3 0.1 copy.32
  4.4 0.1 copy.26
  4.5 0.1 pad_add_fusion
  4.6 0.1 compare_reduce_fusion
  4.8 0.7 %and_convert_fusion.picked_ref = bf16[2,16,128]{2,1,0:T(8,128)(2,1)} fusion(pred[2,16,128]{2,1,0:T(8,128)(4,1)S(1)} %compare_reduce_fusion, s32[128]{0:T(128)S(1)} %fusion.6, s32[2,16]{1,0:T(2,128)S(1)} %pad.4), kind=kLoop, calls=%fused_computation.8 | loop fusion | flops 12288 | bytes 12928 | tf_op jit(solution)/shard_map/convert_element_type | solution.py:388
  5.4 0.0 copy-done.1
  5.4 0.0 copy-done
  5.4 0.2 maximum_bitcast_fusion
  5.6 0.7 %copy.27 = bf16[2,2,128,128]{3,2,1,0:T(8,128)(2,1)} copy(bf16[2,2,128,128]{3,0,2,1:T(2,128)(2,1)S(1)} %maximum_bitcast_fusion) | data formatting | bytes 262144 | tf_op jit(solution)/shard_map/transpose | solution.py:400
  6.3 52.5 %shard_map.76 = (bf16[128,32,128]{2,1,0:T(8,128)(2,1)}, bf16[2,2,2,64,128]{4,3,2,1,0:T(8,128)(2,1)}) custom-call(s32[2,7]{1,0:T(2,128)} %copy-done.5, s32[2,7]{1,0:T(2,128)} %copy-done.4, s32[2,16]{1,0:T(2,128)} %get-tuple-element.16.slot_of, s32[2,16]{1,0:T(2,128)} %copy-done.3, s32[2,16]{1,0:T(2,128)} %copy-done.6, ...), custom_call_target="tpu_custom_call" | custom-call | tf_op jit(solution)/shard_map/pallas_call | solution.py:417
  58.8 0.9 %fusion.7 = (bf16[2,1,128,128]{3,2,1,0:T(8,128)(2,1)S(1)}, bf16[2,1,128,128]{3,2,1,0:T(8,128)(2,1)S(1)}) fusion(bf16[2,2,128,128]{3,2,1,0:T(8,128)(2,1)} %bitcast.18), kind=kLoop, calls=%fused_computation.37 | loop fusion | bytes 262144 | tf_op jit(solution)/shard_map/slice | solution.py:442
  59.7 0.7 %copy.38 = bf16[2,1,128,128]{3,0,2,1:T(2,128)(2,1)} copy(bf16[2,1,128,128]{3,2,1,0:T(8,128)(2,1)S(1)} %get-tuple-element.9) | data formatting | bytes 131072
  60.4 0.7 %copy.39 = bf16[2,1,128,128]{3,0,2,1:T(2,128)(2,1)} copy(bf16[2,1,128,128]{3,2,1,0:T(8,128)(2,1)S(1)} %get-tuple-element.10) | data formatting | bytes 131072
  61.1 2.3 %copy.41 = bf16[128,32,128]{2,1,0:T(8,128)(2,1)} copy(bf16[128,32,128]{2,1,0:T(8,128)(2,1)} %get-tuple-element.20) | data formatting | bytes 2097152
  (9 shorter events, 0.1 us)
Async XLA Ops:
  0.6 0.7 %copy-start.2 = (s32[128,2,8]{0,2,1:T(8,128)S(1)}, s32[128,2,8]{0,2,1:T(8,128)}, u32[]{:S(2)}) copy-start(s32[128,2,8]{0,2,1:T(8,128)} %param.9) | copy-start | bytes 24580
  1.3 4.1 %copy-start.1 = (bf16[128,2,128]{2,1,0:T(2,128)(2,1)S(1)}, bf16[128,2,128]{2,1,0:T(2,128)(2,1)}, u32[]{:S(2)}) copy-start(bf16[128,2,128]{2,1,0:T(2,128)(2,1)} %param.6) | copy-start | bytes 196612
  1.4 4.1 %copy-start = (bf16[128,2,128]{2,1,0:T(2,128)(2,1)S(1)}, bf16[128,2,128]{2,1,0:T(2,128)(2,1)}, u32[]{:S(2)}) copy-start(bf16[128,2,128]{2,1,0:T(2,128)(2,1)} %param.7) | copy-start | bytes 196612
  1.6 0.5 copy-start.3
  3.0 0.6 copy-start.6
  3.7 0.6 copy-start.4
  3.7 0.7 %copy-start.5 = (s32[2,7]{1,0:T(2,128)}, s32[2,7]{1,0:T(2,128)S(1)}, u32[]{:S(2)}) copy-start(s32[2,7]{1,0:T(2,128)S(1)} %get-tuple-element.8.far_owner) | copy-start | bytes 172

commit v3 on v2

--- a/solution.py
+++ b/solution.py
@@ -11,23 +11,10 @@
 BLK = 64
 NEG = -1e30
 ID_ROWS = 16
+LANES = 128
 LOG2E = math.log2(math.e)
 NT = (((1,), (1,)), ((), ()))
 NN = (((1,), (0,)), ((), ()))
-
-
-def barrier_all(n, me):
-    barrier = pltpu.get_barrier_semaphore()
-
-    def greet(k, carry):
-        peer = lax.rem(me + k, n)
-        pl.semaphore_signal(
-            barrier, inc=1, device_id={"ctx": peer}, device_id_type=pl.DeviceIdType.MESH
-        )
-        return carry
-
-    lax.fori_loop(1, n, greet, 0)
-    pl.semaphore_wait(barrier, n - 1)
 
 
 def attend(
@@ -86,12 +73,62 @@
         acc_ref[1] += dv.reshape(slots, BLK, dh)
 
 
-def fill_pool(g, n_far, far_owner, far_block, own_kv, gathered_ref, pool_ref):
+def fill_tables(g, n, me, n_far, own_blocks, sel_ref, picked_ref, tab_ref):
+    sel = sel_ref[g]
+    tokens = sel.shape[1]
+    shift = own_blocks.bit_length() - 1
+    owner = sel >> shift
+    block = sel & (own_blocks - 1)
+    peers = lax.broadcasted_iota(jnp.int32, (n, tokens), 0)
+    code = jnp.zeros((n, tokens), jnp.float32)
+    for i in range(sel.shape[0]):
+        mark = (block[i : i + 1] + 1).astype(jnp.float32)
+        code = jnp.maximum(code, jnp.where(owner[i : i + 1] == peers, mark, 0.0))
+    code = jnp.broadcast_to(jnp.max(code, axis=1, keepdims=True), (n, LANES))
+    peers = lax.broadcasted_iota(jnp.int32, (n, LANES), 0)
+    code = jnp.where(peers == me, 0.0, code)
+    live = jnp.where(code > 0.0, 1.0, 0.0)
+    before = lax.broadcasted_iota(jnp.int32, (n, n), 1) < lax.broadcasted_iota(jnp.int32, (n, n), 0)
+    before = jnp.where(before, 1.0, 0.0).astype(jnp.bfloat16)
+    slot = lax.dot_general(before, live.astype(jnp.bfloat16), NN, preferred_element_type=jnp.float32)
+    far = jnp.maximum(code - 1.0, 0.0)
+    lane = lax.broadcasted_iota(jnp.int32, (n, LANES), 1)
+    kept = jnp.minimum(slot, float(n_far - 1))
+    entry = jnp.where(lane == 0, kept, jnp.where(lane == 1, live, far))
+    tab_ref[g, :n, :] = entry.astype(jnp.int32)
+    peer = peers.astype(jnp.float32)
+    now = me * own_blocks + (lax.broadcasted_iota(jnp.int32, (1, tokens), 1) >> BLK.bit_length() - 1)
+    slots = picked_ref.shape[1]
+    row = lax.broadcasted_iota(jnp.int32, (slots, tokens), 0)
+    far_rows = tab_ref.shape[1] - n
+    far_row = lax.broadcasted_iota(jnp.int32, (far_rows, LANES), 0)
+    far_lane = lax.broadcasted_iota(jnp.int32, (far_rows, LANES), 1)
+    far_entry = jnp.zeros((far_rows, LANES), jnp.float32)
+    picked = jnp.zeros((slots, tokens), jnp.float32)
+    for i in range(own_blocks + n_far):
+        if i < own_blocks:
+            ids = jnp.full((1, tokens), me * own_blocks + i, jnp.int32)
+        else:
+            hit = (live > 0.0) & (slot == float(i - own_blocks))
+            who = jnp.max(jnp.where(hit, peer, -1.0), axis=0, keepdims=True)
+            which = jnp.max(jnp.where(hit, far, 0.0), axis=0, keepdims=True)
+            ids = jnp.max(who * own_blocks + which, axis=1, keepdims=True).astype(jnp.int32)
+            ids = jnp.broadcast_to(ids, (1, tokens))
+            here = jnp.where(far_lane == 0, jnp.maximum(who, 0.0), which)
+            far_entry = jnp.where(far_row == i - own_blocks, here, far_entry)
+        seen = jnp.max(jnp.where(sel == ids, 1.0, 0.0), axis=0, keepdims=True)
+        seen = jnp.where(ids <= now, seen, 0.0)
+        picked = jnp.where(row == i, seen, picked)
+    tab_ref[g, n:, :] = far_entry.astype(jnp.int32)
+    picked_ref[g] = picked.astype(jnp.bfloat16)
+
+
+def fill_pool(g, n, n_far, tab, own_kv, gathered_ref, pool_ref):
     own_rows = own_kv.shape[2] * BLK
     pool_ref[:, :own_rows, :] = own_kv[g].reshape(2, own_rows, own_kv.shape[4])
     for s in range(n_far):
-        owner = far_owner[g, s]
-        block = far_block[g, s]
+        owner = jnp.clip(tab[g, n + s, 0], 0, n - 1)
+        block = jnp.clip(tab[g, n + s, 1], 0, own_kv.shape[2] - 1)
         lo = own_rows + s * BLK
         for kv in range(2):
             pool_ref[kv, lo : lo + BLK, :] = gathered_ref[owner, kv, block]
@@ -99,13 +136,12 @@
 
 def fused_kernel(
     n, cols, n_far, chunk_tokens, groups,
-    far_owner, far_block, slot_of, live, block_of,
-    picked_ref, q_ref, do_ref, own_kv, dq_ref, out_ref, *scratch,
+    sel_ref, q_hbm, do_hbm, own_kv, dq_ref, key_out, value_out, *scratch,
 ):
     per_bank = 9
     banks = [scratch[g * per_bank : (g + 1) * per_bank] for g in range(groups)]
     (
-        pool_ref, mid_ref, col_send, y_send, sib_send, recv_sem,
+        picked_ref, tab_ref, tab, q_ref, do_ref, mix_ref, in_sem, pool_ref, mid_ref, col_send, y_send, sib_send, recv_sem,
         rs_sem, ry_send, ry_recv, rz_send, rz_recv,
     ) = scratch[groups * per_bank :]
     depth = n // (2 * cols)
@@ -119,6 +155,7 @@
     other_y = cols - 1 - y
     y_peer = 2 * (z * cols + other_y) + core
     own_blocks = own_kv.shape[2]
+    own_rows = own_blocks * BLK
     dh = own_kv.shape[4]
     per_group = q_ref.shape[1] // groups
     chunks = q_ref.shape[0] // chunk_tokens
@@ -223,7 +260,7 @@
         )
 
     def far_part(g, dest, kv):
-        return banks[g][1][kv, own_blocks + slot_of[g, dest]]
+        return banks[g][1][kv, own_blocks + jnp.clip(tab[g, dest, 0], 0, n_far - 1)]
 
     def return_start(g):
         acc_ref, box = banks[g][1], banks[g][2]
@@ -232,8 +269,8 @@
         @pl.loop(0, chips)
         def _(q):
             dest = 2 * q + 1 - core
-            keep = live[g, dest].astype(jnp.float32)
-            ids = jnp.full((ID_ROWS, dh), block_of[g, dest].astype(jnp.float32), jnp.float32)
+            keep = tab[g, dest, 1].astype(jnp.float32)
+            ids = jnp.full((ID_ROWS, dh), tab[g, dest, 2].astype(jnp.float32), jnp.float32)
             box[q, :ID_ROWS, :] = ids.astype(jnp.bfloat16)
             for kv in range(2):
                 lo = ID_ROWS + kv * BLK
@@ -246,8 +283,8 @@
         dest = 2 * q + core
         box = banks[g][3]
         which = box[q, :ID_ROWS, :].astype(jnp.float32)[:1]
-        keep = live[g, dest].astype(jnp.float32)
-        block = jnp.full((1, dh), block_of[g, dest].astype(jnp.float32), jnp.float32)
+        keep = tab[g, dest, 1].astype(jnp.float32)
+        block = jnp.full((1, dh), tab[g, dest, 2].astype(jnp.float32), jnp.float32)
         for kv in range(2):
             lo = ID_ROWS + kv * BLK
             theirs = box[q, lo : lo + BLK, :].astype(jnp.float32)
@@ -297,7 +334,9 @@
             z_arrival(g, from_z).wait_recv()
             banks[g][8][...] += banks[g][7][from_z].astype(jnp.float32)
 
-        out_ref[g] = banks[g][8][...].astype(jnp.bfloat16)
+        for kv in range(2):
+            whole = banks[g][8][kv].reshape(own_rows, dh)
+            mix_ref[kv, pl.ds(g, own_rows, stride=groups), :] = whole
 
     def return_drain(g):
         sib_copy(g).wait_send()
@@ -310,11 +349,38 @@
         def _(k):
             z_copy(g, lax.rem(z + k, depth)).wait_send()
 
-    barrier_all(n, me)
+    barrier = pltpu.get_barrier_semaphore()
+
+    def greet(peer):
+        pl.semaphore_signal(
+            barrier, inc=1, device_id={"ctx": peer}, device_id_type=pl.DeviceIdType.MESH
+        )
+
+    @pl.loop(1, depth)
+    def _(k):
+        greet(device(lax.rem(z + k, depth), y, core))
+
+    if cols > 1:
+        greet(y_peer)
+    greet(sib)
+    loads = [
+        pltpu.make_async_copy(q_hbm, q_ref, in_sem.at[0]),
+        pltpu.make_async_copy(do_hbm, do_ref, in_sem.at[1]),
+    ]
+    for load in loads:
+        load.start()
+    pl.semaphore_wait(barrier, depth + cols - 1)
     for g in range(groups):
         gather_start(g)
     for g in range(groups):
+        fill_tables(g, n, me, n_far, own_blocks, sel_ref, picked_ref, tab_ref)
+    to_scalars = pltpu.make_async_copy(tab_ref, tab, in_sem.at[2])
+    to_scalars.start()
+    for g in range(groups):
         banks[g][1][...] = jnp.zeros_like(banks[g][1])
+    to_scalars.wait()
+    for load in loads:
+        load.wait()
     gather_column(0)
     gather_across(0)
     gather_end(0)
@@ -326,7 +392,7 @@
         if g > 0:
             first.append(functools.partial(return_across, g - 1))
             last.append(functools.partial(return_column, g - 1))
-        fill_pool(g, n_far, far_owner, far_block, own_kv, banks[g][0], pool_ref)
+        fill_pool(g, n, n_far, tab, own_kv, banks[g][0], pool_ref)
         cuts = sorted({0, min(1, chunks), chunks // 2, chunks})
         for i in range(len(cuts) - 1):
             attend(
@@ -346,6 +412,8 @@
     for g in range(groups):
         gather_drain(g)
         return_drain(g)
+    key_out[...] = mix_ref[0, : own_rows * groups].astype(jnp.bfloat16)
+    value_out[...] = mix_ref[1, : own_rows * groups].astype(jnp.bfloat16)
 
 
 def columns_of(mesh, n):
@@ -354,38 +422,6 @@
         return 1
     cols = sum(spot[2] == spots[0][2] for spot in spots) // 2
     return 2 if cols == 2 and n % 4 == 0 else 1
-
-
-def tables(selected, tokens, n, fetched):
-    own_blocks = tokens // BLK
-    me = lax.axis_index("ctx")
-    peers = jnp.arange(n, dtype=jnp.int32)
-    owner_of = selected // own_blocks
-    local_of = selected - owner_of * own_blocks
-    match = (owner_of[..., None] == peers) & (peers != me)
-    code = jnp.max(jnp.where(match, local_of[..., None] + 1, 0), axis=(0, 2))
-    live = (code > 0).astype(jnp.int32)
-    block_of = jnp.maximum(code - 1, 0)
-    before = (peers[None, :] < peers[:, None]).astype(jnp.int32)
-    slot = jnp.sum(before[None] * live[:, None, :], axis=2)
-    slot_of = jnp.minimum(slot, fetched - 1)
-    pick = (slot[:, None, :] == jnp.arange(fetched)[None, :, None]) & (live[:, None, :] > 0)
-    far_owner = jnp.sum(jnp.where(pick, peers, 0), axis=2)
-    far_block = jnp.sum(jnp.where(pick, block_of[:, None, :], 0), axis=2)
-    far_live = jnp.any(pick, axis=2)
-    groups = selected.shape[1]
-    own_ids = me * own_blocks + jnp.arange(own_blocks, dtype=jnp.int32)
-    far_ids = jnp.where(far_live, far_owner * own_blocks + far_block, -1)
-    pool = jnp.concatenate(
-        [jnp.broadcast_to(own_ids, (groups, own_blocks)), far_ids], axis=1
-    )
-    pad = -pool.shape[1] % 16
-    pool = jnp.pad(pool, ((0, 0), (0, pad)), constant_values=-1)
-    now = me * own_blocks + jnp.arange(tokens, dtype=jnp.int32) // BLK
-    chosen = selected.transpose(1, 2, 0)
-    picked = jnp.any(chosen[:, None] == pool[:, :, None, None], axis=2)
-    picked = picked & (pool[:, :, None] <= now)
-    return far_owner, far_block, slot_of, live, block_of, picked.astype(jnp.bfloat16)
 
 
 def local(cols, queries, keys, values, grad_out, selected):
@@ -395,13 +431,15 @@
     n = lax.axis_size("ctx")
     depth = n // (2 * cols)
     fetched = min(n - 2, max(selected.shape[2] - own_blocks, 4)) + 1
+    slots = -(-(own_blocks + fetched) // 16) * 16
+    far_rows = -(-fetched // 8) * 8
     pool_rows = (own_blocks + fetched) * BLK
-    far_owner, far_block, slot_of, live, block_of, picked = tables(selected, tokens, n, fetched)
+    chosen = selected.transpose(1, 2, 0)
     own_kv = jnp.stack([keys, values], axis=0).transpose(2, 0, 1, 3)
     piece = (2, own_blocks, BLK, dh)
     own_kv = own_kv.reshape((groups,) + piece)
     vmem = pl.BlockSpec(memory_space=pltpu.VMEM)
-    smem = pl.BlockSpec(memory_space=pltpu.SMEM)
+    any_spec = pl.BlockSpec(memory_space=pl.ANY)
     bank = [
         pltpu.VMEM((n,) + piece, jnp.bfloat16),
         pltpu.VMEM((2, pool_rows // BLK, BLK, dh), jnp.float32),
@@ -414,15 +452,23 @@
         pltpu.VMEM(piece, jnp.float32),
     ]
     dma = pltpu.SemaphoreType.DMA
-    dq, summed = pl.pallas_call(
+    dq, key_grad, value_grad = pl.pallas_call(
         functools.partial(fused_kernel, n, cols, fetched, min(tokens, 32), groups),
         out_shape=(
             jax.ShapeDtypeStruct(queries.shape, jnp.bfloat16),
-            jax.ShapeDtypeStruct((groups,) + piece, jnp.bfloat16),
+            jax.ShapeDtypeStruct((tokens * groups, dh), jnp.bfloat16),
+            jax.ShapeDtypeStruct((tokens * groups, dh), jnp.bfloat16),
         ),
-        in_specs=[smem] * 5 + [vmem] * 4,
-        out_specs=(vmem, vmem),
+        in_specs=[vmem, any_spec, any_spec, vmem],
+        out_specs=(vmem, vmem, vmem),
         scratch_shapes=bank * groups + [
+            pltpu.VMEM((groups, slots, tokens), jnp.bfloat16),
+            pltpu.VMEM((groups, n + far_rows, LANES), jnp.int32),
+            pltpu.SMEM((groups, n + far_rows, LANES), jnp.int32),
+            pltpu.VMEM(queries.shape, jnp.bfloat16),
+            pltpu.VMEM(queries.shape, jnp.bfloat16),
+            pltpu.VMEM((2, tokens * groups + 8, dh), jnp.float32),
+            dma((3,)),
             pltpu.VMEM((2, pool_rows, dh), jnp.bfloat16),
             pltpu.VMEM((depth,) + piece, jnp.float32),
             dma((groups, depth)),
@@ -436,11 +482,8 @@
             dma((groups, depth)),
         ],
         compiler_params=pltpu.CompilerParams(collective_id=0, has_side_effects=True),
-    )(far_owner, far_block, slot_of, live, block_of, picked, queries, grad_out, own_kv)
-    summed = summed.reshape(groups, 2, tokens, dh)
-    key_grad = summed[:, 0].transpose(1, 0, 2)
-    value_grad = summed[:, 1].transpose(1, 0, 2)
-    return dq, key_grad, value_grad
+    )(chosen, queries, grad_out, own_kv)
+    return dq, key_grad.reshape(keys.shape), value_grad.reshape(values.shape)
 
 
 def solution(mesh):

time: 63.7 us -> 58.4 us (0.917)
  local copies, waits for them, and re-layouts: 7.82 us -> 4.46 us
  other arithmetic: 2.29 us -> 1.06 us
    unnamed x19 -> x7, local copies, waits for them, and re-layouts: 6.04 us -> 3.79 us
    slice x1 -> x0, local copies, waits for them, and re-layouts: 0.89 us -> none  [local(): value_grad = summed[:, 1].transpose(1, 0, 2)]
    transpose x1, other arithmetic: 0.18 us -> 1.06 us  [local(): own_kv = jnp.stack([keys, values], axis=0).transpose(2, 0, 1, 3)]
    convert_element_type x2 -> x0, other arithmetic: 0.68 us -> none  [the longest x1 0.68 us: tables(): picked.astype(jnp.bfloat16)]
where the time goes in v3:
time: 58.4 us; the launch traced here: 58.2 us
  Pallas kernels  52 us (89%)
  local copies, waits for them, and re-layouts  4.46 us (8%)
  other arithmetic  1.06 us (2%)
  between operations  0.65 us (1%)
    pallas_call x1, Pallas kernels, local(): pl.pallas_call(functools.partial(fused_kernel, n, cols, fetched, min(toke...  52 us
    unnamed x7, local copies, waits for them, and re-layouts  3.79 us

profile of v3, /device:TPU:0, one launch (start us, length us, event | category | flops | bytes accessed | tf_op | source)
XLA Modules:
  0.0 58.2 jit_solution(17522408615323757775)
XLA Ops:
  0.6 1.1 %maximum_bitcast_fusion = bf16[2,2,128,128]{3,0,2,1:T(2,128)(2,1)S(1)} fusion(bf16[1,128,2,128]{3,2,1,0:T(2,128)(2,1)} %bitcast.11, bf16[1,128,2,128]{3,2,1,0:T(2,128)(2,1)} %bitcast.12), kind=kLoop, calls=%fused_computation | loop fusion | flops 65536 | bytes 262144 | tf_op jit(solution)/shard_map/transpose | solution.py:438
  1.7 0.7 %copy.8 = bf16[2,2,128,128]{3,2,1,0:T(8,128)(2,1)} copy(bf16[2,2,128,128]{3,0,2,1:T(2,128)(2,1)S(1)} %maximum_bitcast_fusion) | data formatting | bytes 262144 | tf_op jit(solution)/shard_map/transpose | solution.py:438
  2.4 52.0 %shard_map.76 = (bf16[128,32,128]{2,1,0:T(8,128)(2,1)}, bf16[256,128]{1,0:T(8,128)(2,1)}, bf16[256,128]{1,0:T(8,128)(2,1)}) custom-call(s32[2,8,128]{2,1,0:T(8,128)} %bitcast.13, bf16[128,32,128]{2,1,0:T(8,128)(2,1)} %q_hbm.1, bf16[128,32,128]{2,1,0:T(8,128)(2,1)} %do_hbm.1, bf16[2,2,2,64,128]{4,3,2,1,0:T(8,128)(2,1)} %bitcast.8), custom_call_target="tpu_custom_call" | custom-call | tf_op jit(solution)/shard_map/pallas_call | solution.py:455
  54.4 0.0 copy-start.1
  54.4 2.3 %copy.12 = bf16[128,32,128]{2,1,0:T(8,128)(2,1)} copy(bf16[128,32,128]{2,1,0:T(8,128)(2,1)} %get-tuple-element.12) | data formatting | bytes 2097152
  56.7 0.0 copy-done.1
  56.7 0.0 copy-start
  56.7 0.6 %copy.13 = bf16[128,2,128]{2,1,0:T(2,128)(2,1)} copy(bf16[128,2,128]{2,1,0:T(2,128)(2,1)S(1)} %bitcast.10) | data formatting | bytes 131072
  57.3 0.2 copy-done
  57.6 0.6 %copy.14 = bf16[128,2,128]{2,1,0:T(2,128)(2,1)} copy(bf16[128,2,128]{2,1,0:T(2,128)(2,1)S(1)} %bitcast.9) | data formatting | bytes 131072
Async XLA Ops:
  54.4 2.3 %copy-start.1 = (bf16[256,128]{1,0:T(8,128)(2,1)S(1)}, bf16[256,128]{1,0:T(8,128)(2,1)}, u32[]{:S(2)}) copy-start(bf16[256,128]{1,0:T(8,128)(2,1)} %get-tuple-element.7) | copy-start | bytes 196612
  56.7 0.9 %copy-start = (bf16[256,128]{1,0:T(8,128)(2,1)S(1)}, bf16[256,128]{1,0:T(8,128)(2,1)}, u32[]{:S(2)}) copy-start(bf16[256,128]{1,0:T(8,128)(2,1)} %get-tuple-element.8) | copy-start | bytes 196612

commit v4 on v3

--- a/solution.py
+++ b/solution.py
@@ -17,60 +17,59 @@
 NN = (((1,), (0,)), ((), ()))
 
 
-def attend(
-    g, per_group, chunk_tokens, lo, hi, picked_ref, q_ref, do_ref, dq_ref, pool_ref, acc_ref
-):
+def weigh(g, per_group, chunk, chunk_tokens, own_slots, picked_ref, q_ref, do_ref, pool_ref, p_ref, acc_ref):
     tokens, _, dh = q_ref.shape
-    own_rows = tokens
     keys = pool_ref.shape[1]
     slots = keys // BLK
-    own_slots = own_rows // BLK
-    scaling = 1.0 / math.sqrt(dh)
-    log_scale = scaling * LOG2E
+    log_scale = LOG2E / math.sqrt(dh)
     rows = chunk_tokens * per_group
     shift = per_group.bit_length() - 1
-    pool_k = pool_ref[0]
-    pool_v = pool_ref[1]
-    pool_kt = pool_k.T
     heads = slice(g * per_group, (g + 1) * per_group)
-
-    @pl.loop(lo, hi)
-    def _(c):
-        t0 = pl.multiple_of(c * chunk_tokens, chunk_tokens)
-        q = q_ref[pl.ds(t0, chunk_tokens), heads, :].reshape(rows, dh)
-        do = do_ref[pl.ds(t0, chunk_tokens), heads, :].reshape(rows, dh)
-        row_tok = t0 + (lax.broadcasted_iota(jnp.int32, (tokens, rows), 1) >> shift)
-        tok = lax.broadcasted_iota(jnp.int32, (tokens, rows), 0)
-        spread = jnp.where(row_tok == tok, 1.0, 0.0).astype(jnp.bfloat16)
-        seen = lax.dot_general(picked_ref[g], spread, NN, preferred_element_type=jnp.float32)
-        bias = (seen - 1.0) * (-NEG)
-        s = lax.dot_general(pool_k, q, NT, preferred_element_type=jnp.float32)
-        dp = lax.dot_general(pool_v, do, NT, preferred_element_type=jnp.float32)
-        pieces = []
-        for j in range(slots):
-            piece = s[j * BLK : (j + 1) * BLK] + bias[j : j + 1]
-            if j < own_slots:
-                key_pos = j * BLK + lax.broadcasted_iota(jnp.int32, (BLK, rows), 0)
-                causal = key_pos <= row_tok[:BLK]
-                piece = jnp.where(causal, piece, NEG)
-            pieces.append(piece)
-        s = jnp.concatenate(pieces, axis=0)
-        peak = jnp.max(s, axis=0, keepdims=True)
-        e = jnp.exp2((s - peak) * log_scale)
-        total = jnp.sum(e, axis=0, keepdims=True)
-        weighted = jnp.sum(e * dp, axis=0, keepdims=True)
-        inv = 1.0 / total
-        inner = weighted * inv
-        p = e * inv
-        ds = (p * (dp - inner)).astype(jnp.bfloat16)
-        p = p.astype(jnp.bfloat16)
-        dqt = lax.dot_general(pool_kt, ds, NN, preferred_element_type=jnp.float32)
-        dq = (dqt * scaling).T.astype(jnp.bfloat16)
-        dq_ref[pl.ds(t0, chunk_tokens), heads, :] = dq.reshape(chunk_tokens, per_group, dh)
-        dk = lax.dot_general(ds, q, NN, preferred_element_type=jnp.float32)
-        dv = lax.dot_general(p, do, NN, preferred_element_type=jnp.float32)
-        acc_ref[0] += dk.reshape(slots, BLK, dh)
-        acc_ref[1] += dv.reshape(slots, BLK, dh)
+    t0 = chunk * chunk_tokens
+    q = q_ref[t0 : t0 + chunk_tokens, heads, :].reshape(rows, dh)
+    do = do_ref[t0 : t0 + chunk_tokens, heads, :].reshape(rows, dh)
+    row_tok = t0 + (lax.broadcasted_iota(jnp.int32, (tokens, rows), 1) >> shift)
+    tok = lax.broadcasted_iota(jnp.int32, (tokens, rows), 0)
+    spread = jnp.where(row_tok == tok, 1.0, 0.0).astype(jnp.bfloat16)
+    seen = lax.dot_general(picked_ref[g], spread, NN, preferred_element_type=jnp.float32)
+    bias = (seen - 1.0) * (-NEG)
+    s = lax.dot_general(pool_ref[0], q, NT, preferred_element_type=jnp.float32)
+    pieces = []
+    for j in range(slots):
+        piece = s[j * BLK : (j + 1) * BLK] + bias[j : j + 1]
+        if j < own_slots:
+            key_pos = j * BLK + lax.broadcasted_iota(jnp.int32, (BLK, rows), 0)
+            piece = jnp.where(key_pos <= row_tok[:BLK], piece, NEG)
+        pieces.append(piece)
+    s = jnp.concatenate(pieces, axis=0)
+    peak = jnp.max(s, axis=0, keepdims=True)
+    e = jnp.exp2((s - peak) * log_scale)
+    p = e * (1.0 / jnp.sum(e, axis=0, keepdims=True))
+    p_ref[chunk] = p
+    dv = lax.dot_general(p.astype(jnp.bfloat16), do, NN, preferred_element_type=jnp.float32)
+    dv = dv.reshape(slots, BLK, dh)
+    acc_ref[...] = dv if chunk == 0 else acc_ref[...] + dv
+
+
+def differentiate(g, per_group, chunk, chunk_tokens, q_ref, do_ref, dq_ref, pool_ref, p_ref, acc_ref):
+    dh = q_ref.shape[2]
+    keys = pool_ref.shape[1]
+    scaling = 1.0 / math.sqrt(dh)
+    rows = chunk_tokens * per_group
+    heads = slice(g * per_group, (g + 1) * per_group)
+    t0 = chunk * chunk_tokens
+    q = q_ref[t0 : t0 + chunk_tokens, heads, :].reshape(rows, dh)
+    do = do_ref[t0 : t0 + chunk_tokens, heads, :].reshape(rows, dh)
+    p = p_ref[chunk]
+    dp = lax.dot_general(pool_ref[1], do, NT, preferred_element_type=jnp.float32)
+    inner = jnp.sum(p * dp, axis=0, keepdims=True)
+    ds = (p * (dp - inner)).astype(jnp.bfloat16)
+    dqt = lax.dot_general(pool_ref[0].T, ds, NN, preferred_element_type=jnp.float32)
+    dq = (dqt * scaling).T.astype(jnp.bfloat16)
+    dq_ref[t0 : t0 + chunk_tokens, heads, :] = dq.reshape(chunk_tokens, per_group, dh)
+    dk = lax.dot_general(ds, q, NN, preferred_element_type=jnp.float32)
+    dk = dk.reshape(keys // BLK, BLK, dh)
+    acc_ref[...] = dk if chunk == 0 else acc_ref[...] + dk
 
 
 def fill_tables(g, n, me, n_far, own_blocks, sel_ref, picked_ref, tab_ref):
@@ -123,27 +122,29 @@
     picked_ref[g] = picked.astype(jnp.bfloat16)
 
 
-def fill_pool(g, n, n_far, tab, own_kv, gathered_ref, pool_ref):
-    own_rows = own_kv.shape[2] * BLK
-    pool_ref[:, :own_rows, :] = own_kv[g].reshape(2, own_rows, own_kv.shape[4])
+def fill_pool(unit, n, n_far, tab, own_kv, gathered_ref, pool_ref):
+    group, kv = divmod(unit, 2)
+    own_blocks = own_kv.shape[1]
+    own_rows = own_blocks * BLK
+    pool_ref[kv, :own_rows, :] = own_kv[unit].reshape(own_rows, own_kv.shape[3])
     for s in range(n_far):
-        owner = jnp.clip(tab[g, n + s, 0], 0, n - 1)
-        block = jnp.clip(tab[g, n + s, 1], 0, own_kv.shape[2] - 1)
+        owner = jnp.clip(tab[group, n + s, 0], 0, n - 1)
+        block = jnp.clip(tab[group, n + s, 1], 0, own_blocks - 1)
         lo = own_rows + s * BLK
-        for kv in range(2):
-            pool_ref[kv, lo : lo + BLK, :] = gathered_ref[owner, kv, block]
+        pool_ref[kv, lo : lo + BLK, :] = gathered_ref[owner, block]
 
 
 def fused_kernel(
     n, cols, n_far, chunk_tokens, groups,
     sel_ref, q_hbm, do_hbm, own_kv, dq_ref, key_out, value_out, *scratch,
 ):
-    per_bank = 9
-    banks = [scratch[g * per_bank : (g + 1) * per_bank] for g in range(groups)]
+    per_bank = 10
+    units = 2 * groups
+    banks = [scratch[g * per_bank : (g + 1) * per_bank] for g in range(units)]
     (
-        picked_ref, tab_ref, tab, q_ref, do_ref, mix_ref, in_sem, pool_ref, mid_ref, col_send, y_send, sib_send, recv_sem,
+        picked_ref, tab_ref, tab, q_ref, do_ref, mix_ref, in_sem, pool_ref, p_ref, col_send, y_send, sib_send, recv_sem,
         rs_sem, ry_send, ry_recv, rz_send, rz_recv,
-    ) = scratch[groups * per_bank :]
+    ) = scratch[units * per_bank :]
     depth = n // (2 * cols)
     chips = n // 2
     me = lax.axis_index("ctx")
@@ -154,9 +155,9 @@
     sib = 2 * chip + 1 - core
     other_y = cols - 1 - y
     y_peer = 2 * (z * cols + other_y) + core
-    own_blocks = own_kv.shape[2]
+    own_blocks = own_kv.shape[1]
     own_rows = own_blocks * BLK
-    dh = own_kv.shape[4]
+    dh = own_kv.shape[3]
     per_group = q_ref.shape[1] // groups
     chunks = q_ref.shape[0] // chunk_tokens
     scaling = 1.0 / math.sqrt(dh)
@@ -259,22 +260,21 @@
             rz_send.at[g, from_z], rz_recv.at[g, from_z], peer,
         )
 
-    def far_part(g, dest, kv):
-        return banks[g][1][kv, own_blocks + jnp.clip(tab[g, dest, 0], 0, n_far - 1)]
+    def far_part(g, dest):
+        return banks[g][1][own_blocks + jnp.clip(tab[g // 2, dest, 0], 0, n_far - 1)]
 
     def return_start(g):
         acc_ref, box = banks[g][1], banks[g][2]
-        acc_ref[0] = acc_ref[0] * scaling
+        if g % 2 == 0:
+            acc_ref[...] = acc_ref[...] * scaling
 
         @pl.loop(0, chips)
         def _(q):
             dest = 2 * q + 1 - core
-            keep = tab[g, dest, 1].astype(jnp.float32)
-            ids = jnp.full((ID_ROWS, dh), tab[g, dest, 2].astype(jnp.float32), jnp.float32)
-            box[q, :ID_ROWS, :] = ids.astype(jnp.bfloat16)
-            for kv in range(2):
-                lo = ID_ROWS + kv * BLK
-                box[q, lo : lo + BLK, :] = (far_part(g, dest, kv) * keep).astype(jnp.bfloat16)
+            keep = tab[g // 2, dest, 1].astype(jnp.float32)
+            block = tab[g // 2, dest, 2].astype(jnp.float32)
+            box[q, :ID_ROWS, :] = jnp.full((ID_ROWS, dh), block, jnp.float32).astype(jnp.bfloat16)
+            box[q, ID_ROWS:, :] = (far_part(g, dest) * keep).astype(jnp.bfloat16)
 
         sib_copy(g).start()
 
@@ -283,17 +283,14 @@
         dest = 2 * q + core
         box = banks[g][3]
         which = box[q, :ID_ROWS, :].astype(jnp.float32)[:1]
-        keep = tab[g, dest, 1].astype(jnp.float32)
-        block = jnp.full((1, dh), tab[g, dest, 2].astype(jnp.float32), jnp.float32)
-        for kv in range(2):
-            lo = ID_ROWS + kv * BLK
-            theirs = box[q, lo : lo + BLK, :].astype(jnp.float32)
-            mine = far_part(g, dest, kv) * keep
-            for b in range(own_blocks):
-                yield kv, b, (
-                    jnp.where(block == float(b), mine, 0.0)
-                    + jnp.where(which == float(b), theirs, 0.0)
-                )
+        keep = tab[g // 2, dest, 1].astype(jnp.float32)
+        block = jnp.full((1, dh), tab[g // 2, dest, 2].astype(jnp.float32), jnp.float32)
+        theirs = box[q, ID_ROWS:, :].astype(jnp.float32)
+        mine = far_part(g, dest) * keep
+        for b in range(own_blocks):
+            yield b, (
+                jnp.where(block == float(b), mine, 0.0) + jnp.where(which == float(b), theirs, 0.0)
+            )
 
     def return_across(g):
         sib_copy(g).wait_recv()
@@ -301,27 +298,27 @@
             @pl.loop(0, depth)
             def _(k):
                 zz = lax.rem(z + 1 + k, depth)
-                for kv, b, part in merged(g, zz, other_y):
-                    banks[g][4][zz, kv, b] = part.astype(jnp.bfloat16)
+                for b, part in merged(g, zz, other_y):
+                    banks[g][4][zz, b] = part.astype(jnp.bfloat16)
                 y_copy(g, zz).start()
 
         @pl.loop(0, depth)
         def _(k):
-            for kv, b, part in merged(g, k, y):
-                mid_ref[k, kv, b] = part
+            for b, part in merged(g, k, y):
+                banks[g][9][k, b] = part
 
     def return_column(g):
         @pl.loop(1, depth)
         def _(k):
             to_z = lax.rem(z + k, depth)
-            total = mid_ref[to_z]
+            total = banks[g][9][to_z]
             if cols > 1:
                 y_copy(g, to_z).wait_recv()
                 total = total + banks[g][5][to_z].astype(jnp.float32)
             banks[g][6][to_z] = total.astype(jnp.bfloat16)
             z_copy(g, to_z).start()
 
-        total = mid_ref[z] + banks[g][1][:, :own_blocks]
+        total = banks[g][9][z] + banks[g][1][:own_blocks]
         if cols > 1:
             y_copy(g, z).wait_recv()
             total = total + banks[g][5][z].astype(jnp.float32)
@@ -334,9 +331,8 @@
             z_arrival(g, from_z).wait_recv()
             banks[g][8][...] += banks[g][7][from_z].astype(jnp.float32)
 
-        for kv in range(2):
-            whole = banks[g][8][kv].reshape(own_rows, dh)
-            mix_ref[kv, pl.ds(g, own_rows, stride=groups), :] = whole
+        whole = banks[g][8][...].reshape(own_rows, dh)
+        mix_ref[g % 2, pl.ds(g // 2, own_rows, stride=groups), :] = whole
 
     def return_drain(g):
         sib_copy(g).wait_send()
@@ -370,48 +366,73 @@
     for load in loads:
         load.start()
     pl.semaphore_wait(barrier, depth + cols - 1)
-    for g in range(groups):
-        gather_start(g)
+    for u in range(units):
+        gather_start(u)
     for g in range(groups):
         fill_tables(g, n, me, n_far, own_blocks, sel_ref, picked_ref, tab_ref)
     to_scalars = pltpu.make_async_copy(tab_ref, tab, in_sem.at[2])
     to_scalars.start()
-    for g in range(groups):
-        banks[g][1][...] = jnp.zeros_like(banks[g][1])
     to_scalars.wait()
     for load in loads:
         load.wait()
     gather_column(0)
     gather_across(0)
     gather_end(0)
+    fill = functools.partial(fill_pool, n=n, n_far=n_far, tab=tab, own_kv=own_kv, pool_ref=pool_ref)
     for g in range(groups):
-        first, last = [], []
+        keys_unit, values_unit = 2 * g, 2 * g + 1
+        fill(keys_unit, gathered_ref=banks[keys_unit][0])
+        if g > 0:
+            return_start(values_unit - 2)
+            return_start(keys_unit - 2)
+        for i in range(chunks):
+            weigh(
+                g, per_group, i, chunk_tokens, own_blocks,
+                picked_ref, q_ref, do_ref, pool_ref, p_ref, banks[values_unit][1],
+            )
+            if i == 0:
+                gather_column(values_unit)
+            if i == min(1, chunks - 1) and g > 0:
+                return_across(values_unit - 2)
+            if i == min(2, chunks - 1):
+                gather_across(values_unit)
+                if g > 0:
+                    return_across(keys_unit - 2)
+        gather_end(values_unit)
+        fill(values_unit, gathered_ref=banks[values_unit][0])
+        if g + 1 == groups:
+            return_start(values_unit)
+        for i in range(chunks):
+            differentiate(
+                g, per_group, i, chunk_tokens,
+                q_ref, do_ref, dq_ref, pool_ref, p_ref, banks[keys_unit][1],
+            )
+            if i == 0:
+                if g > 0:
+                    return_column(values_unit - 2)
+                if g + 1 < groups:
+                    gather_column(keys_unit + 2)
+            if i == min(1, chunks - 1):
+                if g + 1 == groups:
+                    return_across(values_unit)
+                if g > 0:
+                    return_column(keys_unit - 2)
+            if i == min(2, chunks - 1) and g + 1 < groups:
+                gather_across(keys_unit + 2)
         if g + 1 < groups:
-            first.append(functools.partial(gather_column, g + 1))
-            last.append(functools.partial(gather_across, g + 1))
-        if g > 0:
-            first.append(functools.partial(return_across, g - 1))
-            last.append(functools.partial(return_column, g - 1))
-        fill_pool(g, n, n_far, tab, own_kv, banks[g][0], pool_ref)
-        cuts = sorted({0, min(1, chunks), chunks // 2, chunks})
-        for i in range(len(cuts) - 1):
-            attend(
-                g, per_group, chunk_tokens, cuts[i], cuts[i + 1],
-                picked_ref, q_ref, do_ref, dq_ref, pool_ref, banks[g][1],
-            )
-            for step in (first if i == 0 else last if i == len(cuts) - 2 else []):
-                step()
-        if g + 1 < groups:
-            gather_end(g + 1)
-        return_start(g)
-    final = groups - 1
-    return_across(final)
-    return_column(final)
-    for g in range(groups):
-        return_end(g)
-    for g in range(groups):
-        gather_drain(g)
-        return_drain(g)
+            gather_end(keys_unit + 2)
+    last = units - 2
+    return_start(last)
+    return_column(last + 1)
+    return_across(last)
+    for u in range(last):
+        return_end(u)
+    return_column(last)
+    return_end(last + 1)
+    return_end(last)
+    for u in range(units):
+        gather_drain(u)
+        return_drain(u)
     key_out[...] = mix_ref[0, : own_rows * groups].astype(jnp.bfloat16)
     value_out[...] = mix_ref[1, : own_rows * groups].astype(jnp.bfloat16)
 
@@ -431,29 +452,33 @@
     n = lax.axis_size("ctx")
     depth = n // (2 * cols)
     fetched = min(n - 2, max(selected.shape[2] - own_blocks, 4)) + 1
+    chunk_tokens = min(tokens, 32)
+    chunk_rows = chunk_tokens * (head_count // groups)
     slots = -(-(own_blocks + fetched) // 16) * 16
     far_rows = -(-fetched // 8) * 8
     pool_rows = (own_blocks + fetched) * BLK
     chosen = selected.transpose(1, 2, 0)
     own_kv = jnp.stack([keys, values], axis=0).transpose(2, 0, 1, 3)
-    piece = (2, own_blocks, BLK, dh)
-    own_kv = own_kv.reshape((groups,) + piece)
+    piece = (own_blocks, BLK, dh)
+    units = 2 * groups
+    own_kv = own_kv.reshape((units,) + piece)
     vmem = pl.BlockSpec(memory_space=pltpu.VMEM)
     any_spec = pl.BlockSpec(memory_space=pl.ANY)
     bank = [
         pltpu.VMEM((n,) + piece, jnp.bfloat16),
-        pltpu.VMEM((2, pool_rows // BLK, BLK, dh), jnp.float32),
-        pltpu.VMEM((n // 2, ID_ROWS + 2 * BLK, dh), jnp.bfloat16),
-        pltpu.VMEM((n // 2, ID_ROWS + 2 * BLK, dh), jnp.bfloat16),
+        pltpu.VMEM((pool_rows // BLK, BLK, dh), jnp.float32),
+        pltpu.VMEM((n // 2, ID_ROWS + BLK, dh), jnp.bfloat16),
+        pltpu.VMEM((n // 2, ID_ROWS + BLK, dh), jnp.bfloat16),
         pltpu.VMEM((depth,) + piece, jnp.bfloat16),
         pltpu.VMEM((depth,) + piece, jnp.bfloat16),
         pltpu.VMEM((depth,) + piece, jnp.bfloat16),
         pltpu.VMEM((depth,) + piece, jnp.bfloat16),
         pltpu.VMEM(piece, jnp.float32),
+        pltpu.VMEM((depth,) + piece, jnp.float32),
     ]
     dma = pltpu.SemaphoreType.DMA
     dq, key_grad, value_grad = pl.pallas_call(
-        functools.partial(fused_kernel, n, cols, fetched, min(tokens, 32), groups),
+        functools.partial(fused_kernel, n, cols, fetched, chunk_tokens, groups),
         out_shape=(
             jax.ShapeDtypeStruct(queries.shape, jnp.bfloat16),
             jax.ShapeDtypeStruct((tokens * groups, dh), jnp.bfloat16),
@@ -461,7 +486,7 @@
         ),
         in_specs=[vmem, any_spec, any_spec, vmem],
         out_specs=(vmem, vmem, vmem),
-        scratch_shapes=bank * groups + [
+        scratch_shapes=bank * units + [
             pltpu.VMEM((groups, slots, tokens), jnp.bfloat16),
             pltpu.VMEM((groups, n + far_rows, LANES), jnp.int32),
             pltpu.SMEM((groups, n + far_rows, LANES), jnp.int32),
@@ -470,16 +495,16 @@
             pltpu.VMEM((2, tokens * groups + 8, dh), jnp.float32),
             dma((3,)),
             pltpu.VMEM((2, pool_rows, dh), jnp.bfloat16),
-            pltpu.VMEM((depth,) + piece, jnp.float32),
-            dma((groups, depth)),
-            dma((groups, depth)),
-            dma((groups, n)),
-            dma((groups, n)),
-            dma((groups, 2)),
-            dma((groups, depth)),
-            dma((groups, depth)),
-            dma((groups, depth)),
-            dma((groups, depth)),
+            pltpu.VMEM((tokens // chunk_tokens, pool_rows, chunk_rows), jnp.float32),
+            dma((units, depth)),
+            dma((units, depth)),
+            dma((units, n)),
+            dma((units, n)),
+            dma((units, 2)),
+            dma((units, depth)),
+            dma((units, depth)),
+            dma((units, depth)),
+            dma((units, depth)),
         ],
         compiler_params=pltpu.CompilerParams(collective_id=0, has_side_effects=True),
     )(chosen, queries, grad_out, own_kv)

time: 58.4 us -> 59.9 us (1.026)
  Pallas kernels: 52 us -> 53.4 us
    pallas_call x1, Pallas kernels: 52 us -> 53.4 us  [local(): pl.pallas_call(functools.partial(fused_kernel, n, cols, fetched, chunk_to...]
where the time goes in v4:
time: 59.9 us; the launch traced here: 59.6 us
  Pallas kernels  53.4 us (89%)
  local copies, waits for them, and re-layouts  4.46 us (7%)
  other arithmetic  1.06 us (2%)
  between operations  0.65 us (1%)
    pallas_call x1, Pallas kernels, local(): pl.pallas_call(functools.partial(fused_kernel, n, cols, fetched, chunk_to...  53.4 us
    unnamed x7, local copies, waits for them, and re-layouts  3.79 us

profile of v4, /device:TPU:0, one launch (start us, length us, event | category | flops | bytes accessed | tf_op | source)
XLA Modules:
  0.0 59.6 jit_solution(2942874297952426725)
XLA Ops:
  0.6 1.1 %maximum_bitcast_fusion = bf16[2,2,128,128]{3,0,2,1:T(2,128)(2,1)S(1)} fusion(bf16[1,128,2,128]{3,2,1,0:T(2,128)(2,1)} %bitcast.11, bf16[1,128,2,128]{3,2,1,0:T(2,128)(2,1)} %bitcast.12), kind=kLoop, calls=%fused_computation | loop fusion | flops 65536 | bytes 262144 | tf_op jit(solution)/shard_map/transpose | solution.py:461
  1.7 0.7 %copy.8 = bf16[2,2,128,128]{3,2,1,0:T(8,128)(2,1)} copy(bf16[2,2,128,128]{3,0,2,1:T(2,128)(2,1)S(1)} %maximum_bitcast_fusion) | data formatting | bytes 262144 | tf_op jit(solution)/shard_map/transpose | solution.py:461
  2.4 53.4 %shard_map.76 = (bf16[128,32,128]{2,1,0:T(8,128)(2,1)}, bf16[256,128]{1,0:T(8,128)(2,1)}, bf16[256,128]{1,0:T(8,128)(2,1)}) custom-call(s32[2,8,128]{2,1,0:T(8,128)} %bitcast.13, bf16[128,32,128]{2,1,0:T(8,128)(2,1)} %q_hbm.1, bf16[128,32,128]{2,1,0:T(8,128)(2,1)} %do_hbm.1, bf16[4,2,64,128]{3,2,1,0:T(8,128)(2,1)} %bitcast.8), custom_call_target="tpu_custom_call" | custom-call | tf_op jit(solution)/shard_map/pallas_call | solution.py:480
  55.8 0.0 copy-start.1
  55.8 2.3 %copy.12 = bf16[128,32,128]{2,1,0:T(8,128)(2,1)} copy(bf16[128,32,128]{2,1,0:T(8,128)(2,1)} %get-tuple-element.12) | data formatting | bytes 2097152
  58.1 0.0 copy-done.1
  58.1 0.0 copy-start
  58.1 0.6 %copy.13 = bf16[128,2,128]{2,1,0:T(2,128)(2,1)} copy(bf16[128,2,128]{2,1,0:T(2,128)(2,1)S(1)} %bitcast.10) | data formatting | bytes 131072
  58.8 0.2 copy-done
  59.0 0.6 %copy.14 = bf16[128,2,128]{2,1,0:T(2,128)(2,1)} copy(bf16[128,2,128]{2,1,0:T(2,128)(2,1)S(1)} %bitcast.9) | data formatting | bytes 131072
Async XLA Ops:
  55.8 2.3 %copy-start.1 = (bf16[256,128]{1,0:T(8,128)(2,1)S(1)}, bf16[256,128]{1,0:T(8,128)(2,1)}, u32[]{:S(2)}) copy-start(bf16[256,128]{1,0:T(8,128)(2,1)} %get-tuple-element.7) | copy-start | bytes 196612
  58.1 0.9 %copy-start = (bf16[256,128]{1,0:T(8,128)(2,1)S(1)}, bf16[256,128]{1,0:T(8,128)(2,1)}, u32[]{:S(2)}) copy-start(bf16[256,128]{1,0:T(8,128)(2,1)} %get-tuple-element.8) | copy-start | bytes 196612

commit v5 on v4

--- a/solution.py
+++ b/solution.py
@@ -376,54 +376,51 @@
     for load in loads:
         load.wait()
     gather_column(0)
+    gather_column(1)
     gather_across(0)
+    gather_across(1)
     gather_end(0)
     fill = functools.partial(fill_pool, n=n, n_far=n_far, tab=tab, own_kv=own_kv, pool_ref=pool_ref)
     for g in range(groups):
         keys_unit, values_unit = 2 * g, 2 * g + 1
         fill(keys_unit, gathered_ref=banks[keys_unit][0])
-        if g > 0:
-            return_start(values_unit - 2)
-            return_start(keys_unit - 2)
         for i in range(chunks):
             weigh(
                 g, per_group, i, chunk_tokens, own_blocks,
                 picked_ref, q_ref, do_ref, pool_ref, p_ref, banks[values_unit][1],
             )
-            if i == 0:
-                gather_column(values_unit)
-            if i == min(1, chunks - 1) and g > 0:
-                return_across(values_unit - 2)
-            if i == min(2, chunks - 1):
-                gather_across(values_unit)
-                if g > 0:
+            if g + 1 < groups:
+                if i == 0:
+                    gather_column(keys_unit + 2)
+                if i == min(1, chunks - 1):
+                    gather_column(values_unit + 2)
+                if i == min(2, chunks - 1):
+                    gather_across(keys_unit + 2)
+                if i == chunks - 1:
+                    gather_across(values_unit + 2)
+            if g > 0:
+                if i == 0:
                     return_across(keys_unit - 2)
+                    return_column(values_unit - 2)
+                if i == min(2, chunks - 1):
+                    return_column(keys_unit - 2)
         gather_end(values_unit)
         fill(values_unit, gathered_ref=banks[values_unit][0])
-        if g + 1 == groups:
-            return_start(values_unit)
+        return_start(values_unit)
         for i in range(chunks):
             differentiate(
                 g, per_group, i, chunk_tokens,
                 q_ref, do_ref, dq_ref, pool_ref, p_ref, banks[keys_unit][1],
             )
-            if i == 0:
-                if g > 0:
-                    return_column(values_unit - 2)
-                if g + 1 < groups:
-                    gather_column(keys_unit + 2)
             if i == min(1, chunks - 1):
-                if g + 1 == groups:
-                    return_across(values_unit)
-                if g > 0:
-                    return_column(keys_unit - 2)
-            if i == min(2, chunks - 1) and g + 1 < groups:
-                gather_across(keys_unit + 2)
+                return_across(values_unit)
+            if i == chunks - 1 and g + 1 == groups:
+                return_start(keys_unit)
+                return_column(values_unit)
         if g + 1 < groups:
+            return_start(keys_unit)
             gather_end(keys_unit + 2)
     last = units - 2
-    return_start(last)
-    return_column(last + 1)
     return_across(last)
     for u in range(last):
         return_end(u)

time: 59.9 us -> 60.7 us (1.013)
  Pallas kernels: 53.4 us -> 54.2 us
    pallas_call x1, Pallas kernels: 53.4 us -> 54.2 us  [local(): pl.pallas_call(functools.partial(fused_kernel, n, cols, fetched, chunk_to...]
where the time goes in v5:
time: 60.7 us; the launch traced here: 60.4 us
  Pallas kernels  54.2 us (89%)
  local copies, waits for them, and re-layouts  4.46 us (7%)
  other arithmetic  1.06 us (2%)
  between operations  0.65 us (1%)
    pallas_call x1, Pallas kernels, local(): pl.pallas_call(functools.partial(fused_kernel, n, cols, fetched, chunk_to...  54.2 us
    unnamed x7, local copies, waits for them, and re-layouts  3.79 us

profile of v5, /device:TPU:0, one launch (start us, length us, event | category | flops | bytes accessed | tf_op | source)
XLA Modules:
  0.0 60.4 jit_solution(17606730027381377790)
XLA Ops:
  0.6 1.1 %maximum_bitcast_fusion = bf16[2,2,128,128]{3,0,2,1:T(2,128)(2,1)S(1)} fusion(bf16[1,128,2,128]{3,2,1,0:T(2,128)(2,1)} %bitcast.11, bf16[1,128,2,128]{3,2,1,0:T(2,128)(2,1)} %bitcast.12), kind=kLoop, calls=%fused_computation | loop fusion | flops 65536 | bytes 262144 | tf_op jit(solution)/shard_map/transpose | solution.py:458
  1.7 0.7 %copy.8 = bf16[2,2,128,128]{3,2,1,0:T(8,128)(2,1)} copy(bf16[2,2,128,128]{3,0,2,1:T(2,128)(2,1)S(1)} %maximum_bitcast_fusion) | data formatting | bytes 262144 | tf_op jit(solution)/shard_map/transpose | solution.py:458
  2.4 54.2 %shard_map.76 = (bf16[128,32,128]{2,1,0:T(8,128)(2,1)}, bf16[256,128]{1,0:T(8,128)(2,1)}, bf16[256,128]{1,0:T(8,128)(2,1)}) custom-call(s32[2,8,128]{2,1,0:T(8,128)} %bitcast.13, bf16[128,32,128]{2,1,0:T(8,128)(2,1)} %q_hbm.1, bf16[128,32,128]{2,1,0:T(8,128)(2,1)} %do_hbm.1, bf16[4,2,64,128]{3,2,1,0:T(8,128)(2,1)} %bitcast.8), custom_call_target="tpu_custom_call" | custom-call | tf_op jit(solution)/shard_map/pallas_call | solution.py:477
  56.6 0.0 copy-start.1
  56.6 2.3 %copy.12 = bf16[128,32,128]{2,1,0:T(8,128)(2,1)} copy(bf16[128,32,128]{2,1,0:T(8,128)(2,1)} %get-tuple-element.12) | data formatting | bytes 2097152
  58.9 0.0 copy-done.1
  58.9 0.0 copy-start
  58.9 0.6 %copy.13 = bf16[128,2,128]{2,1,0:T(2,128)(2,1)} copy(bf16[128,2,128]{2,1,0:T(2,128)(2,1)S(1)} %bitcast.10) | data formatting | bytes 131072
  59.5 0.2 copy-done
  59.8 0.6 %copy.14 = bf16[128,2,128]{2,1,0:T(2,128)(2,1)} copy(bf16[128,2,128]{2,1,0:T(2,128)(2,1)S(1)} %bitcast.9) | data formatting | bytes 131072
Async XLA Ops:
  56.6 2.3 %copy-start.1 = (bf16[256,128]{1,0:T(8,128)(2,1)S(1)}, bf16[256,128]{1,0:T(8,128)(2,1)}, u32[]{:S(2)}) copy-start(bf16[256,128]{1,0:T(8,128)(2,1)} %get-tuple-element.7) | copy-start | bytes 196612
  58.9 0.9 %copy-start = (bf16[256,128]{1,0:T(8,128)(2,1)S(1)}, bf16[256,128]{1,0:T(8,128)(2,1)}, u32[]{:S(2)}) copy-start(bf16[256,128]{1,0:T(8,128)(2,1)} %get-tuple-element.8) | copy-start | bytes 196612
